TPU v7x, 512 devices: a whole 4x8x8 slice. The times are simulated.
512 devices in a mesh: gx: 8 (over x, core), gy: 8 (over y), gz: 8 (over z).
Axes of the slice: x: 4, y: 8, z: 8, core: 2. Of those that a mesh axis runs over, the one named last changes fastest.
Arguments:
- warped_image: float32 [512, 512, 1024], P('gx', 'gy', 'gz'), may hold values from -6 to 6
- fixed_image: float32 [512, 512, 1024], P('gx', 'gy', 'gz'), may hold values from -6 to 6
- fine_control: float32 [3, 64, 64, 128], P(None, 'gx', 'gy', 'gz'), may hold values from -6 to 6
- coarse_control: float32 [3, 16, 16, 32], replicated, may hold values from -6 to 6
Outputs:
- fine_gradient: float32 [3, 64, 64, 128], P(None, 'gx', 'gy', 'gz')
- coarse_gradient: float32 [3, 16, 16, 32], replicated
All inputs are finite; a program needn't handle non-finite values.
Results may differ from a plain program's by a relative error of at most 0.0003.
Values sent between devices are 32-bit elements; how exact they have to be, the bound alone decides.
No kernel may reach another device: no remote copies, remote signals or barrier semaphores. Data moves between devices by JAX's collectives and lax.ppermute only.
A program may use at most 64 MiB of HBM per device.

v0:
```python
import functools

import jax
import jax.numpy as jnp
import numpy as np
from jax import lax
from jax.experimental import pallas as pl
from jax.experimental.pallas import tpu as pltpu
from jax.sharding import PartitionSpec as P

SPF = 8
SPC = 32
BEND = 0.01
f32 = jnp.float32
bf16 = jnp.bfloat16
VMEM = pltpu.VMEM


def spline(t):
    t = np.abs(t)
    inner = 2.0 / 3.0 - t * t + 0.5 * t**3
    outer = (2.0 - t) ** 3 / 6.0
    return np.where(t < 1.0, inner, np.where(t < 2.0, outer, 0.0))


def weights(voxels, points, spacing):
    centre = (np.arange(points) - 2) * spacing + spacing / 2
    return spline((np.asarray(voxels)[:, None] + 0.5 - centre[None, :]) / spacing)


def halves(matrix):
    matrix = np.asarray(matrix, np.float32)
    high = matrix.astype(bf16)
    return high, (matrix - high.astype(np.float32)).astype(bf16)


def split(values):
    high = values.astype(bf16)
    return high, (values - high.astype(f32)).astype(bf16)


def mm(a, b):
    return jnp.dot(a, b, preferred_element_type=f32)


def mm3(values, high, low):
    a, b = split(values)
    return mm(a, high) + mm(b, high) + mm(a, low)


def lanes(shape):
    return lax.broadcasted_iota(jnp.int32, shape, len(shape) - 1)


def rows_of(shape):
    return lax.broadcasted_iota(jnp.int32, shape, len(shape) - 2)


def rolled(values, shift):
    shift %= values.shape[-1]
    return values if shift == 0 else pltpu.roll(values, shift, values.ndim - 1)


def whole(n):
    return [pl.BlockSpec(memory_space=VMEM)] * n


STEP = 16


def faces_kernel(w_ref, f_ref, xf_ref, yf_ref, zf_ref):
    g = pl.program_id(0)
    lane = lanes((64, 128))
    packed_s = jnp.zeros((64, 128), f32)
    packed_d = jnp.zeros((64, 128), f32)
    for i in range(STEP):
        w = w_ref[i]
        f = f_ref[i]
        s = w + f
        d = w - f
        yf_ref[i, 0:2, :] = s[62:64]
        yf_ref[i, 2:4, :] = d[62:64]
        here = (lane >= 4 * i) & (lane < 4 * i + 4)
        packed_s = jnp.where(here, rolled(s, 4 * i + 2), packed_s)
        packed_d = jnp.where(here, rolled(d, 4 * i + 2), packed_d)
        if i >= STEP - 2:

            @pl.when(g == 3)
            def _():
                xf_ref[i - (STEP - 2)] = s
                xf_ref[2 + i - (STEP - 2)] = d

    half = g // 2

    @pl.when(g % 2 == 0)
    def _():
        zf_ref[half] = packed_s
        zf_ref[2 + half] = packed_d

    @pl.when(g % 2 == 1)
    def _():
        zf_ref[half] = jnp.where(lane < 64, zf_ref[half], rolled(packed_s, 64))
        zf_ref[2 + half] = jnp.where(lane < 64, zf_ref[2 + half], rolled(packed_d, 64))


def faces(w, f):
    block = pl.BlockSpec((STEP, 64, 128), lambda g: (g, 0, 0))
    fixed = pl.BlockSpec((4, 64, 128), lambda g: (0, 0, 0))
    return pl.pallas_call(
        faces_kernel,
        grid=(64 // STEP,),
        in_specs=[block, block],
        out_specs=[fixed, pl.BlockSpec((STEP, 4, 128), lambda g: (g, 0, 0)), fixed],
        out_shape=[
            jax.ShapeDtypeStruct((4, 64, 128), f32),
            jax.ShapeDtypeStruct((64, 4, 128), f32),
            jax.ShapeDtypeStruct((4, 64, 128), f32),
        ],
        name="faces",
    )(w, f)


def bend_kernel(sizes, c_ref, k_ref, bf_ref, bk_ref, u_ref, a_ref, b_ref):
    nx, ny, nz = sizes
    ix, iy, iz = (lax.axis_index(n) for n in ("gx", "gy", "gz"))
    u_ref[...] = jnp.zeros_like(u_ref)
    for a in range(3):
        for p in range(8):
            at = 20 * (p + 2) + 2
            u_ref[a * 16 + 2 : a * 16 + 10, at : at + 16] = c_ref[a, p]
    lane = lanes((48, 256))
    row = rows_of((48, 256)) % 16
    gp = lane // 20 - 2 + 8 * ix
    gr = lane % 20 - 2 + 16 * iz
    gq = row - 2 + 8 * iy
    inside = (gp >= 0) & (gp < 8 * nx) & (gq >= 0) & (gq < 8 * ny) & (gr >= 0) & (gr < 16 * nz)

    def around(u):
        total = pltpu.roll(u, 1, 0) + pltpu.roll(u, 47, 0)
        for shift in (1, 255, 20, 236):
            total = total + pltpu.roll(u, shift, 1)
        return total - 6.0 * u

    u = around(u_ref[...])
    u = around(jnp.where(inside, u, 0.0)) * BEND
    keep = lanes((48, 128)) < 120
    bf_ref[:, 0:128] = jnp.where(keep, u[:, 0:128], 0.0)
    bf_ref[:, 128:256] = jnp.where(keep, pltpu.roll(u, 136, 1)[:, 0:128], 0.0)

    kx, ky, kz = 2 * nx, 2 * ny, 4 * nz
    a_ref[...] = jnp.zeros_like(a_ref)
    b_ref[...] = jnp.zeros_like(b_ref)
    for a in range(3):
        for p in range(kx):
            a_ref[a, p + 1, 8 : 8 + ky, 0:kz] = k_ref[a, p]
    grid = lanes((ky, 128)) < kz

    def star(ref, a, p):
        mid = ref[a, p + 1, 8 : 8 + ky, :]
        total = ref[a, p, 8 : 8 + ky, :] + ref[a, p + 2, 8 : 8 + ky, :]
        total = total + ref[a, p + 1, 7 : 7 + ky, :] + ref[a, p + 1, 9 : 9 + ky, :]
        total = total + rolled(mid, 1) + rolled(mid, 127)
        return total - 6.0 * mid

    for a in range(3):
        for p in range(kx):
            b_ref[a, p + 1, 8 : 8 + ky, :] = jnp.where(grid, star(a_ref, a, p), 0.0)
    for a in range(3):
        for p in range(kx):
            bk_ref[a, p] = (star(b_ref, a, p) * BEND)[:, 0:kz]


def bend(sizes, control, coarse):
    nx, ny, nz = sizes
    grid = (3, 2 * nx + 2, 2 * ny + 16, 128)
    return pl.pallas_call(
        functools.partial(bend_kernel, sizes),
        in_specs=whole(2),
        out_specs=whole(2),
        out_shape=[
            jax.ShapeDtypeStruct((48, 256), f32),
            jax.ShapeDtypeStruct(coarse.shape, f32),
        ],
        scratch_shapes=[VMEM((48, 256), f32), VMEM(grid, f32), VMEM(grid, f32)],
        cost_estimate=pl.CostEstimate(flops=4000000, bytes_accessed=1000000, transcendentals=0),
        name="bend",
    )(control, coarse)


@functools.cache
def tables():
    own = np.arange(64)
    cross = np.arange(-2, 2)
    wy = np.zeros((24, 64))
    wy[0:12] = weights(own, 12, SPF).T
    wy[16:22] = weights(own, 6, SPC).T
    high, low = halves(wy)
    left = np.concatenate(
        [np.concatenate([high, high], 1), np.concatenate([low, np.zeros_like(low)], 1)], 0
    )
    wc = np.zeros((8, 8, 128), np.float32)
    for j in range(4):
        wc[j, :, :] = weights(cross, 12, SPF)[j, 0:8, None]
        wc[4 + j, 0:6, :] = weights(cross, 6, SPC)[j, :, None]
    fine_scale = SPF**-1.5 / 24.0
    coarse_scale = SPC**-1.5 / 24.0
    wz = np.zeros((2, 128, 128))
    wz[0, :, 0:20] = weights(np.arange(128), 20, SPF) * fine_scale
    wz[1, :, 0:8] = weights(np.arange(128), 8, SPC) * coarse_scale
    wz_high, wz_low = halves(wz)
    m = np.zeros((2, 128, 384))
    fx, cx = weights(own, 12, SPF), weights(own, 6, SPC)
    fz = weights(cross, 20, SPF) * fine_scale
    cz = weights(cross, 8, SPC) * coarse_scale
    for x in range(64):
        for j in range(4):
            line = m[x // 32, 4 * (x % 32) + j]
            for p in range(12):
                at = 128 * (p // 6) + 20 * (p % 6)
                line[at : at + 20] = fx[x, p] * fz[j]
            for p in range(6):
                at = 256 + 80 + 8 * p
                line[at : at + 8] = cx[x, p] * cz[j]
    m_high, m_low = halves(m)
    coarse_x = weights(own, 6, SPC).astype(np.float32).reshape(-1)
    return left, wc, wz_high, wz_low, m_high, m_low, coarse_x


def project_kernel(
    w_ref, f_ref, xr_ref, yr_ref, zr_ref, zo_ref, bf_ref, left_ref, wc_ref, wzh_ref, wzl_ref, mh_ref, ml_ref, cx_ref,
    chunk_ref, fine_ref, s_ref, tf_ref, tc_ref, af_ref, ac_ref,
):
    n = chunk_ref.shape[0]
    fx = weights(np.arange(8), 5, SPF)
    edge_f = weights(np.arange(-2, 0), 4, SPF)
    edge_c = weights(np.arange(-2, 0), 4, SPC)

    s_ref[:, 0:8, :] = jnp.zeros((68, 8, 128), f32)
    s_ref[:, 72:80, :] = jnp.zeros((68, 8, 128), f32)
    s_ref[66:68, 8:72, :] = jnp.zeros((2, 64, 128), f32)
    s_ref[0:2, 8:72, :] = xr_ref[0:2]

    def add(x, carry):
        s_ref[x + 2, 8:72, :] = w_ref[x] + f_ref[x]
        return carry

    lax.fori_loop(0, 64, add, 0, unroll=8)

    left = left_ref[...]
    lane = lanes((64, 128))

    def along_y(force):
        high, low = split(force)
        both = mm(left, jnp.concatenate([high, low], 0))
        return both[0:24] + both[24:48]

    def layer(x, carry):
        s = s_ref[x + 2, 8:72, :]
        d = w_ref[x] - f_ref[x]
        below, above = s_ref[x + 1, 8:72, :], s_ref[x + 3, 8:72, :]
        f0 = (s_ref[x, 8:72, :] - s_ref[x + 4, 8:72, :]) + 8.0 * (above - below)
        f1 = (s_ref[x + 2, 6:70, :] - s_ref[x + 2, 10:74, :]) + 8.0 * (
            s_ref[x + 2, 9:73, :] - s_ref[x + 2, 7:71, :]
        )
        f2 = jnp.where(lane >= 2, rolled(s, 2), 0.0) - jnp.where(lane < 126, rolled(s, 126), 0.0)
        f2 = f2 + 8.0 * (
            jnp.where(lane < 127, rolled(s, 127), 0.0) - jnp.where(lane >= 1, rolled(s, 1), 0.0)
        )
        t = along_y(jnp.concatenate([f0 * d, f1 * d, f2 * d], 1))
        s0, s1 = s_ref[x + 2, 8:9, :], s_ref[x + 2, 9:10, :]
        d0, d1 = d[0:1], d[1:2]
        sm2, sm1 = yr_ref[x, 0:1, :], yr_ref[x, 1:2, :]
        dm2, dm1 = yr_ref[x, 2:3, :], yr_ref[x, 3:4, :]
        products = (-s0 * dm2, (8.0 * s0 - s1) * dm1, (sm2 - 8.0 * sm1) * d0, sm1 * d1)
        fine = t[0:8, 128:256]
        coarse = t[16:24, 128:256]
        for j in range(4):
            spread = jnp.broadcast_to(products[j], (8, 128))
            fine = fine + wc_ref[j] * spread
            coarse = coarse + wc_ref[4 + j] * spread
        for a in range(3):
            cols = slice(128 * a, 128 * a + 128)
            tf_ref[x, 16 * a : 16 * a + 8, :] = fine if a == 1 else t[0:8, cols]
            tf_ref[x, 16 * a + 8 : 16 * a + 16, :] = t[8:16, cols]
            tc_ref[x, 8 * a : 8 * a + 8, :] = coarse if a == 1 else t[16:24, cols]
        return carry

    lax.fori_loop(0, 64, layer, 0, unroll=2)

    af_ref[...] = jnp.zeros_like(af_ref)
    ac_ref[...] = jnp.zeros_like(ac_ref)

    s0, s1 = s_ref[2, 8:72, :], s_ref[3, 8:72, :]
    edge = along_y(jnp.concatenate([-s0 * xr_ref[2], (8.0 * s0 - s1) * xr_ref[3]], 1))
    for k in range(4):
        af_ref[k, 0:16, :] = float(edge_f[0, k]) * edge[0:16, 0:128] + float(edge_f[1, k]) * edge[0:16, 128:256]
        ac_ref[k, 0:8, :] = float(edge_c[0, k]) * edge[16:24, 0:128] + float(edge_c[1, k]) * edge[16:24, 128:256]

    def block(b, carry):
        for k in range(5):
            total = None
            for r in range(8):
                weight = float(fx[r, k])
                if weight == 0.0:
                    continue
                term = weight * tf_ref[8 * b + r]
                total = term if total is None else total + term
            af_ref[b + k] += total
        for k in range(6):
            total = None
            for r in range(8):
                term = cx_ref[(8 * b + r) * 6 + k] * tc_ref[8 * b + r]
                total = term if total is None else total + term
            ac_ref[k] += total
        return carry

    lax.fori_loop(0, 8, block, 0)

    zf = mm3(af_ref[...].reshape(576, 128), wzh_ref[0], wzl_ref[0])
    zc = mm3(ac_ref[...].reshape(144, 128), wzh_ref[1], wzl_ref[1])
    fine = []
    for h in range(2):
        total = zf[288 * h : 288 * h + 48]
        for i in range(1, 6):
            total = total + rolled(zf[48 * (6 * h + i) : 48 * (6 * h + i) + 48], 20 * i)
        fine.append(total + bf_ref[:, 128 * h : 128 * h + 128])
    coarse = rolled(zc[0:24], 80)
    for p in range(1, 6):
        coarse = coarse + rolled(zc[24 * p : 24 * p + 24], 80 + 8 * p)

    j = lane % 4
    extra = None
    for h in range(2):
        s = jnp.where(j < 2, zr_ref[h], zo_ref[h])
        d = jnp.where(j < 2, zr_ref[2 + h], zo_ref[2 + h])
        slope = jnp.where(j >= 2, rolled(s, 2), 0.0) - jnp.where(j < 2, rolled(s, 126), 0.0)
        slope = slope + 8.0 * (
            jnp.where(j == 1, rolled(s, 127), 0.0) - jnp.where(j == 2, rolled(s, 1), 0.0)
        )
        part = mm3(along_y(slope * d), mh_ref[h], ml_ref[h])
        extra = part if extra is None else extra + part

    zero8 = jnp.zeros((8, 128), f32)
    zero32 = jnp.zeros((32, 128), f32)
    low = fine[0] + jnp.concatenate([zero32, extra[0:16, 0:128]], 0)
    high = fine[1] + jnp.concatenate([zero32, extra[0:16, 128:256]], 0)
    spread = jnp.concatenate(
        [coarse[0:8], zero8, coarse[8:16], zero8, coarse[16:24] + extra[16:24, 256:384], zero8], 0
    )
    fine_ref[:, 0:128] = low
    fine_ref[:, 128:256] = high
    lane = lanes((48, 128))
    chunk = jnp.where(lane < 40, low, jnp.where(lane < 80, rolled(high, 88), spread))
    for i in range(n):
        chunk_ref[i] = chunk


def project(n, w, f, xr, yr, zr, zo, bent):
    constants = tables()
    return pl.pallas_call(
        project_kernel,
        in_specs=whole(13) + [pl.BlockSpec(memory_space=pltpu.SMEM)],
        out_specs=whole(2),
        out_shape=[
            jax.ShapeDtypeStruct((n, 48, 128), f32),
            jax.ShapeDtypeStruct((48, 256), f32),
        ],
        scratch_shapes=[
            VMEM((68, 80, 128), f32),
            VMEM((64, 48, 128), f32),
            VMEM((64, 24, 128), f32),
            VMEM((12, 48, 128), f32),
            VMEM((6, 24, 128), f32),
        ],
        name="project",
    )(w, f, xr, yr, zr, zo, bent, *(jnp.asarray(c) for c in constants))


def sides(ref, axis):
    n = ref.shape[0]
    i = lax.axis_index(axis)
    return ref[jnp.maximum(i - 1, 0)], i > 0, ref[jnp.minimum(i + 1, n - 1)], i < n - 1


def x_kernel(ny, got_ref, fine_ref, chunk_ref, own_ref, pack_ref):
    n = got_ref.shape[0]
    lane = lanes((24, 128))
    coarse = jnp.zeros((24, 128), f32)
    for j in range(n):
        part = jnp.concatenate([got_ref[j, 16 * a : 16 * a + 8, :] for a in range(3)], 0)
        first, last = max(0, 16 * j - 16), min(16 * n, 16 * j + 32)
        coarse = coarse + jnp.where((lane >= first) & (lane < last), rolled(part, 16 * j - 96), 0.0)
    low, has_low, high, has_high = sides(got_ref, "gx")
    lane = lanes((48, 128))
    middle = (lane >= 40) & (lane < 80)
    own_ref[:, 0:128] = fine_ref[:, 0:128] + jnp.where(middle & has_low, low, 0.0)
    own_ref[:, 128:256] = fine_ref[:, 128:256] + jnp.where(middle & has_high, rolled(high, 40), 0.0)
    pack_ref[0:24, :] = coarse
    for h in range(2):
        for a in range(3):
            at = 24 + 12 * h + 4 * a
            cols = slice(128 * h, 128 * h + 128)
            pack_ref[at : at + 2, :] = own_ref[16 * a : 16 * a + 2, cols]
            pack_ref[at + 2 : at + 4, :] = own_ref[16 * a + 10 : 16 * a + 12, cols]
    for i in range(ny):
        chunk_ref[i] = pack_ref[...]


def x_stage(ny, got, fine):
    return pl.pallas_call(
        functools.partial(x_kernel, ny),
        in_specs=whole(2),
        out_specs=whole(2),
        out_shape=[
            jax.ShapeDtypeStruct((ny, 48, 128), f32),
            jax.ShapeDtypeStruct((48, 256), f32),
        ],
        scratch_shapes=[VMEM((48, 128), f32)],
        name="xstage",
    )(got, fine)


def lane_of(p):
    return 128 * (p // 6), 20 * (p % 6)


def y_kernel(nz, got_ref, fine_ref, chunk_ref, own_ref, sum_ref):
    n = got_ref.shape[0]
    sum_ref[...] = jnp.zeros_like(sum_ref)
    for j in range(n):
        for a in range(3):
            at = 24 * a + 2 * j
            sum_ref[at : at + 6, :] += got_ref[j, 8 * a : 8 * a + 6, :]
    low, has_low, high, has_high = sides(got_ref, "gy")
    own_ref[...] = fine_ref[...]
    for h in range(2):
        cols = slice(128 * h, 128 * h + 128)
        for a in range(3):
            at = 24 + 12 * h + 4 * a
            own_ref[16 * a + 2 : 16 * a + 4, cols] += jnp.where(has_low, low[at + 2 : at + 4], 0.0)
            own_ref[16 * a + 8 : 16 * a + 10, cols] += jnp.where(has_high, high[at : at + 2], 0.0)
    lane = lanes((8, 128))
    border = jnp.zeros((8, 128), f32)
    for a in range(3):
        for p in range(8):
            tile, base = lane_of(p + 2)
            v = own_ref[16 * a + 2 : 16 * a + 10, tile : tile + 128]
            at = 32 * a + 4 * p
            border = jnp.where((lane >= at) & (lane < at + 2), rolled(v, at - base), border)
            border = jnp.where((lane >= at + 2) & (lane < at + 4), rolled(v, at - base - 16), border)
    for i in range(nz):
        for a in range(3):
            chunk_ref[i, 16 * a : 16 * a + 16, :] = sum_ref[24 * a + 2 : 24 * a + 18, :]
        chunk_ref[i, 48:56, :] = border


def y_stage(nz, got, fine):
    return pl.pallas_call(
        functools.partial(y_kernel, nz),
        in_specs=whole(2),
        out_specs=whole(2),
        out_shape=[
            jax.ShapeDtypeStruct((nz, 56, 128), f32),
            jax.ShapeDtypeStruct((48, 256), f32),
        ],
        scratch_shapes=[VMEM((72, 128), f32)],
        name="ystage",
    )(got, fine)


def z_kernel(nx, ny, got_ref, fine_ref, bk_ref, out_fine_ref, out_coarse_ref):
    n = got_ref.shape[0]
    low, has_low, high, has_high = sides(got_ref, "gz")
    low = jnp.where(has_low, low[48:56], 0.0)
    high = jnp.where(has_high, high[48:56], 0.0)
    lane = lanes((8, 128))
    for a in range(3):
        for p in range(8):
            tile, base = lane_of(p + 2)
            v = fine_ref[16 * a + 2 : 16 * a + 10, tile : tile + 128]
            at = 32 * a + 4 * p
            v = v + jnp.where((lane >= base + 2) & (lane < base + 4), rolled(low, base - at), 0.0)
            v = v + jnp.where((lane >= base + 16) & (lane < base + 18), rolled(high, base + 16 - at), 0.0)
            out_fine_ref[a, p] = rolled(v, -(base + 2))[:, 0:16]

    lane = lanes((48, 128))
    k = lane % 8
    parts = [got_ref[m, 0:48, :] for m in range(n)]
    sums = []
    for m in range(n):
        total = parts[m]
        if m > 0:
            total = total + jnp.where(k < 4, rolled(parts[m - 1], -4), 0.0)
        if m < n - 1:
            total = total + jnp.where(k >= 4, rolled(parts[m + 1], 4), 0.0)
        sums.append(jnp.where((k >= 2) & (k < 6), total, 0.0))
    tiles = [rolled(sums[2 * m], -2) + rolled(sums[2 * m + 1], 2) for m in range(n // 2)]
    for p in range(2 * nx):
        total = None
        for m in range(n // 2):
            moved = rolled(tiles[m], 8 * m - 8 * p)
            total = moved if total is None else jnp.where(lane >= 8 * m, moved, total)
        for a in range(3):
            out_coarse_ref[a, p] = total[16 * a : 16 * a + 2 * ny, 0 : 4 * n] + bk_ref[a, p]


def z_stage(nx, ny, got, fine, bent):
    return pl.pallas_call(
        functools.partial(z_kernel, nx, ny),
        in_specs=whole(3),
        out_specs=whole(2),
        out_shape=[
            jax.ShapeDtypeStruct((3, 8, 8, 16), f32),
            jax.ShapeDtypeStruct(bent.shape, f32),
        ],
        name="zstage",
    )(got, fine, bent)


def shifted_up(values, axis):
    return lax.ppermute(values, axis, [(i, i + 1) for i in range(lax.axis_size(axis) - 1)])


def exchanged(chunks, axis):
    return lax.all_to_all(chunks, axis, split_axis=0, concat_axis=0, tiled=True)


def per_device(warped_image, fixed_image, fine_control, coarse_control):
    sizes = tuple(lax.axis_size(n) for n in ("gx", "gy", "gz"))
    xf, yf, zf = faces(warped_image, fixed_image)
    zr = shifted_up(zf, "gz")
    yr = shifted_up(yf, "gy")
    xr = shifted_up(xf, "gx")
    bent_fine, bent_coarse = bend(sizes, fine_control, coarse_control)
    chunk, fine = project(sizes[0], warped_image, fixed_image, xr, yr, zr, zf, bent_fine)
    chunk, fine = x_stage(sizes[1], exchanged(chunk, "gx"), fine)
    chunk, fine = y_stage(sizes[2], exchanged(chunk, "gy"), fine)
    return tuple(z_stage(sizes[0], sizes[1], exchanged(chunk, "gz"), fine, bent_coarse))


def solution(mesh):
    in_specs = (P("gx", "gy", "gz"), P("gx", "gy", "gz"), P(None, "gx", "gy", "gz"), P())
    out_specs = (P(None, "gx", "gy", "gz"), P())
    return jax.shard_map(
        per_device, mesh=mesh, in_specs=in_specs, out_specs=out_specs, check_vma=False
    )
```

profile of v0, /device:TPU:2, one launch (start us, length us, event | category | flops | bytes accessed | tf_op | source)
XLA Modules:
  0.0 88.7 jit_solution(3520731324675474644)
XLA Ops:
  0.6 4.7 %faces.1 = (f32[4,64,128]{2,1,0:T(8,128)}, f32[64,4,128]{2,1,0:T(4,128)}, f32[4,64,128]{2,1,0:T(8,128)}) custom-call(f32[64,64,128]{2,1,0:T(8,128)} %w_ref.3, f32[64,64,128]{2,1,0:T(8,128)} %f_ref.3), custom_call_target="tpu_custom_call" | custom-call | tf_op jit(solution)/shard_map/faces/pallas_call | solution.py:109
  5.3 1.9 %collective-permute-start = (f32[4,64,128]{2,1,0:T(8,128)}, f32[4,64,128]{2,1,0:T(8,128)S(1)}, u32[]{:S(2)}, u32[]{:S(2)}) collective-permute-start(f32[4,64,128]{2,1,0:T(8,128)} %get-tuple-element.13), channel_id=1, source_target_pairs={{0,64},{64,128},{128,192},{192,256},{256,320},{320,384},{384,448},... | collective-permute-start | bytes 393224 | tf_op jit(solution)/shard_map/ppermute | solution.py:521
  7.3 3.5 %collective-permute-start.1 = (f32[64,4,128]{2,1,0:T(4,128)}, f32[64,4,128]{2,1,0:T(4,128)S(1)}, u32[]{:S(2)}, u32[]{:S(2)}) collective-permute-start(f32[64,4,128]{2,1,0:T(4,128)} %get-tuple-element.14), channel_id=1, source_target_pairs={{0,8},{8,16},{16,24},{24,32},{32,40},{40,48},{48,56},{1,9},{9,17},... | collective-permute-start | bytes 393224 | tf_op jit(solution)/shard_map/ppermute | solution.py:521
  10.7 4.3 %collective-permute-start.2 = (f32[4,64,128]{2,1,0:T(8,128)}, f32[4,64,128]{2,1,0:T(8,128)S(1)}, u32[]{:S(2)}, u32[]{:S(2)}) collective-permute-start(f32[4,64,128]{2,1,0:T(8,128)} %get-tuple-element.15.zo_ref), channel_id=1, source_target_pairs={{0,1},{1,2},{2,3},{3,4},{4,5},{5,6},{6,7},{8,9},{9,10},{10,11},{11... | collective-permute-start | bytes 393224 | tf_op jit(solution)/shard_map/ppermute | solution.py:521
  15.0 2.6 %bend.1 = (f32[48,256]{1,0:T(8,128)}, f32[3,16,16,32]{3,2,1,0:T(8,128)}) custom-call(f32[3,8,8,16]{3,2,1,0:T(8,128)} %c_ref.1, f32[3,16,16,32]{3,2,1,0:T(8,128)} %k_ref.1), custom_call_target="tpu_custom_call" | custom-call | flops 4000000 | bytes 1000000 | tf_op jit(solution)/shard_map/bend/pallas_call | solution.py:176
  17.6 0.0 collective-permute-done.xr_ref
  17.6 0.0 copy-start
  17.6 0.0 collective-permute-done.1.yr_ref
  17.6 0.0 copy-start.1
  17.6 1.3 %collective-permute-done.2.zr_ref = f32[4,64,128]{2,1,0:T(8,128)S(1)} collective-permute-done((f32[4,64,128]{2,1,0:T(8,128)}, f32[4,64,128]{2,1,0:T(8,128)S(1)}, u32[]{:S(2)}, u32[]{:S(2)}) %collective-permute-start.2) | collective-permute-done | bytes 131104 | tf_op jit(solution)/shard_map/ppermute | solution.py:521
  18.9 0.0 copy-start.2
  18.9 0.0 copy-done
  18.9 0.0 copy-done.1
  18.9 0.7 copy-done.2
  19.5 14.2 %project.1 = (f32[8,48,128]{2,1,0:T(8,128)}, f32[48,256]{1,0:T(8,128)}) custom-call(f32[64,64,128]{2,1,0:T(8,128)} %w_ref.3, f32[64,64,128]{2,1,0:T(8,128)} %f_ref.3, f32[4,64,128]{2,1,0:T(8,128)} %copy-done, f32[64,4,128]{2,1,0:T(4,128)} %copy-done.1, f32[4,64,128]{2,1,0:T(8,128)} %copy-done.2, f32[4,64,128]{2,1,0:T(8,128)} %get-tuple-element.15.zo_ref, ...), custom_call_target="tpu_custom_call" | custom-call | tf_op jit(solution)/shard_map/project/pallas_call | solution.py:360
  33.7 10.6 %all_to_all.15.got_ref = f32[8,48,128]{2,1,0:T(8,128)} all-to-all(f32[8,48,128]{2,1,0:T(8,128)} %get-tuple-element.17), channel_id=1, replica_groups=mesh['gx'=8,'gy'=8,'gz'=8] {'gx'}, dimensions={0} | all-to-all | bytes 393216 | tf_op jit(solution)/shard_map/all_to_all | solution.py:525
  44.3 1.7 %xstage.1 = (f32[8,48,128]{2,1,0:T(8,128)}, f32[48,256]{1,0:T(8,128)}) custom-call(f32[8,48,128]{2,1,0:T(8,128)} %all_to_all.15.got_ref, f32[48,256]{1,0:T(8,128)} %get-tuple-element.18.fine_ref), custom_call_target="tpu_custom_call" | custom-call | tf_op jit(solution)/shard_map/xstage/pallas_call | solution.py:410
  46.0 16.5 %all_to_all.16.got_ref = f32[8,48,128]{2,1,0:T(8,128)} all-to-all(f32[8,48,128]{2,1,0:T(8,128)} %get-tuple-element.19), channel_id=1, replica_groups=mesh['gx'=8,'gy'=8,'gz'=8] {'gy'}, dimensions={0} | all-to-all | bytes 393216 | tf_op jit(solution)/shard_map/all_to_all | solution.py:525
  62.5 1.8 %ystage.1 = (f32[8,56,128]{2,1,0:T(8,128)}, f32[48,256]{1,0:T(8,128)}) custom-call(f32[8,48,128]{2,1,0:T(8,128)} %all_to_all.16.got_ref, f32[48,256]{1,0:T(8,128)} %get-tuple-element.20.fine_ref), custom_call_target="tpu_custom_call" | custom-call | tf_op jit(solution)/shard_map/ystage/pallas_call | solution.py:458
  64.3 21.7 %all_to_all.17.got_ref = f32[8,56,128]{2,1,0:T(8,128)} all-to-all(f32[8,56,128]{2,1,0:T(8,128)} %get-tuple-element.21), channel_id=1, replica_groups=mesh['gx'=8,'gy'=8,'gz'=8] {'gz'}, dimensions={0} | all-to-all | bytes 458752 | tf_op jit(solution)/shard_map/all_to_all | solution.py:525
  86.0 2.6 %zstage.1 = (f32[3,8,8,16]{3,2,1,0:T(8,128)}, f32[3,16,16,32]{3,2,1,0:T(8,128)}) custom-call(f32[8,56,128]{2,1,0:T(8,128)} %all_to_all.17.got_ref, f32[48,256]{1,0:T(8,128)} %get-tuple-element.22.fine_ref, f32[3,16,16,32]{3,2,1,0:T(8,128)} %get-tuple-element.23.bk_ref), custom_call_target="tpu_custom_call" | custom-call | tf_op jit(solution)/shard_map/zstage/pallas_call | solution.py:508
Async XLA Ops:
  5.3 12.3 %collective-permute-start = (f32[4,64,128]{2,1,0:T(8,128)}, f32[4,64,128]{2,1,0:T(8,128)S(1)}, u32[]{:S(2)}, u32[]{:S(2)}) collective-permute-start(f32[4,64,128]{2,1,0:T(8,128)} %get-tuple-element.13), channel_id=1, source_target_pairs={{0,64},{64,128},{128,192},{192,256},{256,320},{320,384},{384,448},... | collective-permute-start | bytes 393224 | tf_op jit(solution)/shard_map/ppermute | solution.py:521
  7.3 10.4 %collective-permute-start.1 = (f32[64,4,128]{2,1,0:T(4,128)}, f32[64,4,128]{2,1,0:T(4,128)S(1)}, u32[]{:S(2)}, u32[]{:S(2)}) collective-permute-start(f32[64,4,128]{2,1,0:T(4,128)} %get-tuple-element.14), channel_id=1, source_target_pairs={{0,8},{8,16},{16,24},{24,32},{32,40},{40,48},{48,56},{1,9},{9,17},... | collective-permute-start | bytes 393224 | tf_op jit(solution)/shard_map/ppermute | solution.py:521
  10.7 8.1 %collective-permute-start.2 = (f32[4,64,128]{2,1,0:T(8,128)}, f32[4,64,128]{2,1,0:T(8,128)S(1)}, u32[]{:S(2)}, u32[]{:S(2)}) collective-permute-start(f32[4,64,128]{2,1,0:T(8,128)} %get-tuple-element.15.zo_ref), channel_id=1, source_target_pairs={{0,1},{1,2},{2,3},{3,4},{4,5},{5,6},{6,7},{8,9},{9,10},{10,11},{11... | collective-permute-start | bytes 393224 | tf_op jit(solution)/shard_map/ppermute | solution.py:521
  17.6 1.3 %copy-start = (f32[4,64,128]{2,1,0:T(8,128)}, f32[4,64,128]{2,1,0:T(8,128)S(1)}, u32[]{:S(2)}) copy-start(f32[4,64,128]{2,1,0:T(8,128)S(1)} %collective-permute-done.xr_ref) | copy-start | bytes 393220
  17.6 1.3 %copy-start.1 = (f32[64,4,128]{2,1,0:T(4,128)}, f32[64,4,128]{2,1,0:T(4,128)S(1)}, u32[]{:S(2)}) copy-start(f32[64,4,128]{2,1,0:T(4,128)S(1)} %collective-permute-done.1.yr_ref) | copy-start | bytes 393220
  18.9 0.7 copy-start.2
where the time goes:
time: 89.3 us; the launch traced here: 88.7 us
  blocking collectives  48.8 us (55%)
  Pallas kernels  27.6 us (31%)
  starting transfers between devices  9.68 us (11%)
  waiting for transfers between devices  1.26 us (1%)
    all_to_all x3, blocking collectives, exchanged(): return lax.all_to_all(chunks, axis, split_axis=0, concat_axis=0, tiled=True)  48.8 us
    pallas_call x1, Pallas kernels, project(): pl.pallas_call(project_kernel, in_specs=whole(13) + [pl.BlockSpec(memory_...  14.2 us
    ppermute x3, starting transfers between devices, shifted_up(): lax.ppermute(values, axis, [(i, i + 1) for i in range(lax.axis_size(axis)...  9.68 us
    pallas_call x1, Pallas kernels, faces(): pl.pallas_call(faces_kernel, grid=(64 // STEP,), in_specs=[block, block],...  4.71 us
    pallas_call x1, Pallas kernels, z_stage(): pl.pallas_call(functools.partial(z_kernel, nx, ny), in_specs=whole(3), ou...  2.64 us
    pallas_call x1, Pallas kernels, bend(): pl.pallas_call(functools.partial(bend_kernel, sizes), in_specs=whole(2),...  2.56 us
  transfers between devices with their start and end apart: 3, of which 1 were waited for; matrix products, arithmetic and copies ran while one was open for 0% of the time, Pallas kernels for 3%

commit v1 on v0

--- a/solution.py
+++ b/solution.py
@@ -61,63 +61,94 @@
     return values if shift == 0 else pltpu.roll(values, shift, values.ndim - 1)
 
 
+def within(mib):
+    return pltpu.CompilerParams(vmem_limit_bytes=mib * 2**20)
+
+
 def whole(n):
     return [pl.BlockSpec(memory_space=VMEM)] * n
 
 
 STEP = 16
-
-
-def faces_kernel(w_ref, f_ref, xf_ref, yf_ref, zf_ref):
-    g = pl.program_id(0)
+PARTS = 64 // STEP
+
+
+def faces_kernel(w_hbm, f_hbm, xf_ref, xo_ref, yf_ref, yo_ref, zf_ref, s_ref, d_ref, w_ref, f_ref, sem):
+    def copies(g):
+        part = pl.ds(g * STEP, STEP)
+        return [
+            pltpu.make_async_copy(hbm.at[part], ref.at[part], sem.at[i, g])
+            for i, (hbm, ref) in enumerate(((w_hbm, w_ref), (f_hbm, f_ref)))
+        ]
+
+    for g in range(PARTS):
+        for copy in copies(g):
+            copy.start()
     lane = lanes((64, 128))
-    packed_s = jnp.zeros((64, 128), f32)
-    packed_d = jnp.zeros((64, 128), f32)
-    for i in range(STEP):
-        w = w_ref[i]
-        f = f_ref[i]
-        s = w + f
-        d = w - f
-        yf_ref[i, 0:2, :] = s[62:64]
-        yf_ref[i, 2:4, :] = d[62:64]
-        here = (lane >= 4 * i) & (lane < 4 * i + 4)
-        packed_s = jnp.where(here, rolled(s, 4 * i + 2), packed_s)
-        packed_d = jnp.where(here, rolled(d, 4 * i + 2), packed_d)
-        if i >= STEP - 2:
-
-            @pl.when(g == 3)
-            def _():
-                xf_ref[i - (STEP - 2)] = s
-                xf_ref[2 + i - (STEP - 2)] = d
-
-    half = g // 2
-
-    @pl.when(g % 2 == 0)
-    def _():
-        zf_ref[half] = packed_s
-        zf_ref[2 + half] = packed_d
-
-    @pl.when(g % 2 == 1)
-    def _():
-        zf_ref[half] = jnp.where(lane < 64, zf_ref[half], rolled(packed_s, 64))
-        zf_ref[2 + half] = jnp.where(lane < 64, zf_ref[2 + half], rolled(packed_d, 64))
+    s_ref[:, 0:8, :] = jnp.zeros((68, 8, 128), f32)
+    s_ref[:, 72:80, :] = jnp.zeros((68, 8, 128), f32)
+    for x in (0, 1, 66, 67):
+        s_ref[x, 8:72, :] = jnp.zeros((64, 128), f32)
+
+    def part(g, carry):
+        for copy in copies(g):
+            copy.wait()
+        packed_s = jnp.zeros((64, 128), f32)
+        packed_d = jnp.zeros((64, 128), f32)
+        for i in range(STEP):
+            x = g * STEP + i
+            w = w_ref[x]
+            f = f_ref[x]
+            s = w + f
+            d = w - f
+            s_ref[x + 2, 8:72, :] = s
+            d_ref[x] = d
+            row = pl.ds(x, 1)
+            for j in range(2):
+                yf_ref[j, row, :] = s[62 + j : 63 + j]
+                yf_ref[2 + j, row, :] = d[62 + j : 63 + j]
+                yo_ref[j, row, :] = s[j : j + 1]
+                yo_ref[2 + j, row, :] = d[j : j + 1]
+            here = (lane >= 4 * i) & (lane < 4 * i + 4)
+            packed_s = jnp.where(here, rolled(s, 4 * i + 2), packed_s)
+            packed_d = jnp.where(here, rolled(d, 4 * i + 2), packed_d)
+        half = g // 2
+
+        @pl.when(g % 2 == 0)
+        def _():
+            zf_ref[half] = packed_s
+            zf_ref[2 + half] = packed_d
+
+        @pl.when(g % 2 == 1)
+        def _():
+            zf_ref[half] = jnp.where(lane < 64, zf_ref[half], rolled(packed_s, 64))
+            zf_ref[2 + half] = jnp.where(lane < 64, zf_ref[2 + half], rolled(packed_d, 64))
+
+        return carry
+
+    lax.fori_loop(0, PARTS, part, 0)
+    for j in range(2):
+        xf_ref[j] = s_ref[64 + j, 8:72, :]
+        xf_ref[2 + j] = d_ref[62 + j]
+        xo_ref[j] = s_ref[2 + j, 8:72, :]
+        xo_ref[2 + j] = d_ref[j]
 
 
 def faces(w, f):
-    block = pl.BlockSpec((STEP, 64, 128), lambda g: (g, 0, 0))
-    fixed = pl.BlockSpec((4, 64, 128), lambda g: (0, 0, 0))
+    shapes = [(4, 64, 128)] * 5 + [(68, 80, 128), (64, 64, 128)]
     return pl.pallas_call(
         faces_kernel,
-        grid=(64 // STEP,),
-        in_specs=[block, block],
-        out_specs=[fixed, pl.BlockSpec((STEP, 4, 128), lambda g: (g, 0, 0)), fixed],
-        out_shape=[
-            jax.ShapeDtypeStruct((4, 64, 128), f32),
-            jax.ShapeDtypeStruct((64, 4, 128), f32),
-            jax.ShapeDtypeStruct((4, 64, 128), f32),
+        in_specs=[pl.BlockSpec(memory_space=pltpu.HBM)] * 2,
+        out_specs=whole(7),
+        out_shape=[jax.ShapeDtypeStruct(s, f32) for s in shapes],
+        scratch_shapes=[
+            VMEM((64, 64, 128), f32),
+            VMEM((64, 64, 128), f32),
+            pltpu.SemaphoreType.DMA((2, PARTS)),
         ],
+        compiler_params=within(16),
         name="faces",
-    )(w, f)
+    )(*(pltpu.with_memory_space_constraint(v, pltpu.HBM) for v in (w, f)))
 
 
 def bend_kernel(sizes, c_ref, k_ref, bf_ref, bk_ref, u_ref, a_ref, b_ref):
@@ -183,6 +214,7 @@
         ],
         scratch_shapes=[VMEM((48, 256), f32), VMEM(grid, f32), VMEM(grid, f32)],
         cost_estimate=pl.CostEstimate(flops=4000000, bytes_accessed=1000000, transcendentals=0),
+        compiler_params=within(8),
         name="bend",
     )(control, coarse)
 
@@ -226,37 +258,20 @@
     return left, wc, wz_high, wz_low, m_high, m_low, coarse_x
 
 
-def project_kernel(
-    w_ref, f_ref, xr_ref, yr_ref, zr_ref, zo_ref, bf_ref, left_ref, wc_ref, wzh_ref, wzl_ref, mh_ref, ml_ref, cx_ref,
-    chunk_ref, fine_ref, s_ref, tf_ref, tc_ref, af_ref, ac_ref,
-):
-    n = chunk_ref.shape[0]
+def along(left, force):
+    high, low = split(force)
+    both = mm(left, jnp.concatenate([high, low], 0))
+    return both[0:24] + both[24:48]
+
+
+def interior_kernel(s_ref, d_ref, left_ref, cx_ref, af_ref, ac_ref, tf_ref, tc_ref):
     fx = weights(np.arange(8), 5, SPF)
-    edge_f = weights(np.arange(-2, 0), 4, SPF)
-    edge_c = weights(np.arange(-2, 0), 4, SPC)
-
-    s_ref[:, 0:8, :] = jnp.zeros((68, 8, 128), f32)
-    s_ref[:, 72:80, :] = jnp.zeros((68, 8, 128), f32)
-    s_ref[66:68, 8:72, :] = jnp.zeros((2, 64, 128), f32)
-    s_ref[0:2, 8:72, :] = xr_ref[0:2]
-
-    def add(x, carry):
-        s_ref[x + 2, 8:72, :] = w_ref[x] + f_ref[x]
-        return carry
-
-    lax.fori_loop(0, 64, add, 0, unroll=8)
-
     left = left_ref[...]
     lane = lanes((64, 128))
 
-    def along_y(force):
-        high, low = split(force)
-        both = mm(left, jnp.concatenate([high, low], 0))
-        return both[0:24] + both[24:48]
-
     def layer(x, carry):
         s = s_ref[x + 2, 8:72, :]
-        d = w_ref[x] - f_ref[x]
+        d = d_ref[x]
         below, above = s_ref[x + 1, 8:72, :], s_ref[x + 3, 8:72, :]
         f0 = (s_ref[x, 8:72, :] - s_ref[x + 4, 8:72, :]) + 8.0 * (above - below)
         f1 = (s_ref[x + 2, 6:70, :] - s_ref[x + 2, 10:74, :]) + 8.0 * (
@@ -266,35 +281,17 @@
         f2 = f2 + 8.0 * (
             jnp.where(lane < 127, rolled(s, 127), 0.0) - jnp.where(lane >= 1, rolled(s, 1), 0.0)
         )
-        t = along_y(jnp.concatenate([f0 * d, f1 * d, f2 * d], 1))
-        s0, s1 = s_ref[x + 2, 8:9, :], s_ref[x + 2, 9:10, :]
-        d0, d1 = d[0:1], d[1:2]
-        sm2, sm1 = yr_ref[x, 0:1, :], yr_ref[x, 1:2, :]
-        dm2, dm1 = yr_ref[x, 2:3, :], yr_ref[x, 3:4, :]
-        products = (-s0 * dm2, (8.0 * s0 - s1) * dm1, (sm2 - 8.0 * sm1) * d0, sm1 * d1)
-        fine = t[0:8, 128:256]
-        coarse = t[16:24, 128:256]
-        for j in range(4):
-            spread = jnp.broadcast_to(products[j], (8, 128))
-            fine = fine + wc_ref[j] * spread
-            coarse = coarse + wc_ref[4 + j] * spread
+        t = along(left, jnp.concatenate([f0 * d, f1 * d, f2 * d], 1))
         for a in range(3):
             cols = slice(128 * a, 128 * a + 128)
-            tf_ref[x, 16 * a : 16 * a + 8, :] = fine if a == 1 else t[0:8, cols]
-            tf_ref[x, 16 * a + 8 : 16 * a + 16, :] = t[8:16, cols]
-            tc_ref[x, 8 * a : 8 * a + 8, :] = coarse if a == 1 else t[16:24, cols]
+            tf_ref[x, 16 * a : 16 * a + 16, :] = t[0:16, cols]
+            tc_ref[x, 8 * a : 8 * a + 8, :] = t[16:24, cols]
         return carry
 
-    lax.fori_loop(0, 64, layer, 0, unroll=2)
+    lax.fori_loop(0, 64, layer, 0, unroll=8)
 
     af_ref[...] = jnp.zeros_like(af_ref)
     ac_ref[...] = jnp.zeros_like(ac_ref)
-
-    s0, s1 = s_ref[2, 8:72, :], s_ref[3, 8:72, :]
-    edge = along_y(jnp.concatenate([-s0 * xr_ref[2], (8.0 * s0 - s1) * xr_ref[3]], 1))
-    for k in range(4):
-        af_ref[k, 0:16, :] = float(edge_f[0, k]) * edge[0:16, 0:128] + float(edge_f[1, k]) * edge[0:16, 128:256]
-        ac_ref[k, 0:8, :] = float(edge_c[0, k]) * edge[16:24, 0:128] + float(edge_c[1, k]) * edge[16:24, 128:256]
 
     def block(b, carry):
         for k in range(5):
@@ -316,8 +313,67 @@
 
     lax.fori_loop(0, 8, block, 0)
 
-    zf = mm3(af_ref[...].reshape(576, 128), wzh_ref[0], wzl_ref[0])
-    zc = mm3(ac_ref[...].reshape(144, 128), wzh_ref[1], wzl_ref[1])
+
+def interior(s, d):
+    left, *_, coarse_x = tables()
+    return pl.pallas_call(
+        interior_kernel,
+        in_specs=whole(3) + [pl.BlockSpec(memory_space=pltpu.SMEM)],
+        out_specs=whole(2),
+        out_shape=[
+            jax.ShapeDtypeStruct((12, 48, 128), f32),
+            jax.ShapeDtypeStruct((6, 24, 128), f32),
+        ],
+        scratch_shapes=[VMEM((64, 48, 128), f32), VMEM((64, 24, 128), f32)],
+        cost_estimate=pl.CostEstimate(flops=40000000, bytes_accessed=4000000, transcendentals=0),
+        compiler_params=within(16),
+        name="interior",
+    )(s, d, jnp.asarray(left), jnp.asarray(coarse_x))
+
+
+def crossing(first, second):
+    sm2, sm1, dm2, dm1 = (first[i] for i in range(4))
+    s0, s1, d0, d1 = (second[i] for i in range(4))
+    return [-s0 * dm2, (8.0 * s0 - s1) * dm1, (sm2 - 8.0 * sm1) * d0, sm1 * d1]
+
+
+def finish_kernel(
+    af_ref, ac_ref, xr_ref, xo_ref, yr_ref, yo_ref, zr_ref, zo_ref, bf_ref, left_ref, wc_ref, wzh_ref, wzl_ref, mh_ref, ml_ref,
+    chunk_ref, fine_ref, sf_ref, sc_ref,
+):
+    n = chunk_ref.shape[0]
+    edge_f = weights(np.arange(-2, 2), 4, SPF)
+    edge_c = weights(np.arange(-2, 2), 4, SPC)
+    left = left_ref[...]
+    lane = lanes((64, 128))
+
+    edge = along(left, jnp.concatenate(crossing(xr_ref, xo_ref), 1))
+    sf_ref[...] = af_ref[...]
+    sc_ref[...] = ac_ref[...]
+    for k in range(4):
+        for j in range(4):
+            cols = slice(128 * j, 128 * j + 128)
+            fine = float(edge_f[j, k]) * edge[0:16, cols]
+            coarse = float(edge_c[j, k]) * edge[16:24, cols]
+            total_f = fine if j == 0 else total_f + fine
+            total_c = coarse if j == 0 else total_c + coarse
+        sf_ref[k, 0:16, :] += total_f
+        sc_ref[k, 0:8, :] += total_c
+
+    edge = along(left, jnp.concatenate(crossing(yr_ref, yo_ref), 1))
+    for p in range(12):
+        total = sf_ref[p, 16:24, :]
+        for j in range(4):
+            total = total + wc_ref[j] * edge[p : p + 1, 128 * j : 128 * j + 128]
+        sf_ref[p, 16:24, :] = total
+    for p in range(6):
+        total = sc_ref[p, 8:16, :]
+        for j in range(4):
+            total = total + wc_ref[4 + j] * edge[16 + p : 17 + p, 128 * j : 128 * j + 128]
+        sc_ref[p, 8:16, :] = total
+
+    zf = mm3(sf_ref[...].reshape(576, 128), wzh_ref[0], wzl_ref[0])
+    zc = mm3(sc_ref[...].reshape(144, 128), wzh_ref[1], wzl_ref[1])
     fine = []
     for h in range(2):
         total = zf[288 * h : 288 * h + 48]
@@ -337,7 +393,7 @@
         slope = slope + 8.0 * (
             jnp.where(j == 1, rolled(s, 127), 0.0) - jnp.where(j == 2, rolled(s, 1), 0.0)
         )
-        part = mm3(along_y(slope * d), mh_ref[h], ml_ref[h])
+        part = mm3(along(left, slope * d), mh_ref[h], ml_ref[h])
         extra = part if extra is None else extra + part
 
     zero8 = jnp.zeros((8, 128), f32)
@@ -355,25 +411,20 @@
         chunk_ref[i] = chunk
 
 
-def project(n, w, f, xr, yr, zr, zo, bent):
-    constants = tables()
+def finish(n, *values):
+    constants = tables()[:-1]
     return pl.pallas_call(
-        project_kernel,
-        in_specs=whole(13) + [pl.BlockSpec(memory_space=pltpu.SMEM)],
+        finish_kernel,
+        in_specs=whole(15),
         out_specs=whole(2),
         out_shape=[
             jax.ShapeDtypeStruct((n, 48, 128), f32),
             jax.ShapeDtypeStruct((48, 256), f32),
         ],
-        scratch_shapes=[
-            VMEM((68, 80, 128), f32),
-            VMEM((64, 48, 128), f32),
-            VMEM((64, 24, 128), f32),
-            VMEM((12, 48, 128), f32),
-            VMEM((6, 24, 128), f32),
-        ],
-        name="project",
-    )(w, f, xr, yr, zr, zo, bent, *(jnp.asarray(c) for c in constants))
+        scratch_shapes=[VMEM((12, 48, 128), f32), VMEM((6, 24, 128), f32)],
+        compiler_params=within(12),
+        name="finish",
+    )(*values, *(jnp.asarray(c) for c in constants))
 
 
 def sides(ref, axis):
@@ -416,6 +467,7 @@
             jax.ShapeDtypeStruct((48, 256), f32),
         ],
         scratch_shapes=[VMEM((48, 128), f32)],
+        compiler_params=within(4),
         name="xstage",
     )(got, fine)
 
@@ -464,6 +516,7 @@
             jax.ShapeDtypeStruct((48, 256), f32),
         ],
         scratch_shapes=[VMEM((72, 128), f32)],
+        compiler_params=within(4),
         name="ystage",
     )(got, fine)
 
@@ -513,6 +566,7 @@
             jax.ShapeDtypeStruct((3, 8, 8, 16), f32),
             jax.ShapeDtypeStruct(bent.shape, f32),
         ],
+        compiler_params=within(6),
         name="zstage",
     )(got, fine, bent)
 
@@ -527,12 +581,13 @@
 
 def per_device(warped_image, fixed_image, fine_control, coarse_control):
     sizes = tuple(lax.axis_size(n) for n in ("gx", "gy", "gz"))
-    xf, yf, zf = faces(warped_image, fixed_image)
+    xf, xo, yf, yo, zf, s, d = faces(warped_image, fixed_image)
     zr = shifted_up(zf, "gz")
     yr = shifted_up(yf, "gy")
     xr = shifted_up(xf, "gx")
     bent_fine, bent_coarse = bend(sizes, fine_control, coarse_control)
-    chunk, fine = project(sizes[0], warped_image, fixed_image, xr, yr, zr, zf, bent_fine)
+    fine, coarse = interior(s, d)
+    chunk, fine = finish(sizes[0], fine, coarse, xr, xo, yr, yo, zr, zf, bent_fine)
     chunk, fine = x_stage(sizes[1], exchanged(chunk, "gx"), fine)
     chunk, fine = y_stage(sizes[2], exchanged(chunk, "gy"), fine)
     return tuple(z_stage(sizes[0], sizes[1], exchanged(chunk, "gz"), fine, bent_coarse))

time: 89.3 us -> 68.7 us (0.77)
  Pallas kernels: 27.6 us -> 11.7 us
  blocking collectives: 48.8 us -> 46.1 us
  waiting for transfers between devices: 1.26 us -> 0.01 us
    pallas_call x2 -> x3, Pallas kernels: 18.9 us -> 9.23 us  [the longest x1 5.49 us: interior(): pl.pallas_call(interior_kernel, in_specs=whole(3) + [pl.BlockSpec(memory_...]
    all_to_all x3, blocking collectives: 48.8 us -> 46.1 us  [exchanged(): return lax.all_to_all(chunks, axis, split_axis=0, concat_axis=0, tiled=True)]
    pallas_call x1, Pallas kernels: 2.56 us -> 0.76 us  [bend(): pl.pallas_call(functools.partial(bend_kernel, sizes), in_specs=whole(2),...]
    pallas_call x1, Pallas kernels: 1.78 us -> 0.16 us  [y_stage(): pl.pallas_call(functools.partial(y_kernel, nz), in_specs=whole(2), out_sp...]
    pallas_call x1, Pallas kernels: 1.72 us -> 0.11 us  [x_stage(): pl.pallas_call(functools.partial(x_kernel, ny), in_specs=whole(2), out_sp...]
    ppermute x3, waiting for transfers between devices: 1.26 us -> 0.01 us  [shifted_up(): lax.ppermute(values, axis, [(i, i + 1) for i in range(lax.axis_size(axis)...]
    pallas_call x1, Pallas kernels: 2.64 us -> 1.49 us  [z_stage(): pl.pallas_call(functools.partial(z_kernel, nx, ny), in_specs=whole(3), ou...]
  transfers between devices with their start and end apart: 3 -> 3, of which waited for: 1 -> 0; matrix products, arithmetic and copies ran while one was open for 0% -> 0% of each run, Pallas kernels for 3% -> 9%
where the time goes in v1:
time: 68.7 us; the launch traced here: 68.5 us
  blocking collectives  46.1 us (67%)
  Pallas kernels  11.7 us (17%)
  starting transfers between devices  9.69 us (14%)
  between operations  0.85 us (1%)
    all_to_all x3, blocking collectives, exchanged(): return lax.all_to_all(chunks, axis, split_axis=0, concat_axis=0, tiled=True)  46.1 us
    ppermute x3, starting transfers between devices, shifted_up(): lax.ppermute(values, axis, [(i, i + 1) for i in range(lax.axis_size(axis)...  9.69 us
    pallas_call x1, Pallas kernels, interior(): pl.pallas_call(interior_kernel, in_specs=whole(3) + [pl.BlockSpec(memory_...  5.49 us
    pallas_call x1, Pallas kernels, faces(): pl.pallas_call(faces_kernel, in_specs=[pl.BlockSpec(memory_space=pltpu.HB...  2.93 us
    pallas_call x1, Pallas kernels, z_stage(): pl.pallas_call(functools.partial(z_kernel, nx, ny), in_specs=whole(3), ou...  1.49 us
  transfers between devices with their start and end apart: 3, of which 0 were waited for; matrix products, arithmetic and copies ran while one was open for 0% of the time, Pallas kernels for 9%

profile of v1, /device:TPU:2, one launch (start us, length us, event | category | flops | bytes accessed | tf_op | source)
XLA Modules:
  0.0 68.5 jit_solution(11569073519506115822)
XLA Ops:
  0.6 0.0 copy-start.6
  0.6 0.0 copy-start.8
  0.7 0.0 copy-start.3
  0.7 0.0 copy-start
  0.7 2.9 %faces.1 = (f32[4,64,128]{2,1,0:T(8,128)S(1)}, f32[4,64,128]{2,1,0:T(8,128)S(1)}, f32[4,64,128]{2,1,0:T(8,128)S(1)}, f32[4,64,128]{2,1,0:T(8,128)S(1)}, f32[4,64...) custom-call(f32[64,64,128]{2,1,0:T(8,128)} %w_hbm.1, f32[64,64,128]{2,1,0:T(8,128)} %f_hbm.1), custom_call_target="tpu_custom_call" | custom-call | tf_op jit(solution)/shard_map/faces/pallas_call | solution.py:139
  3.6 4.3 %collective-permute-start.2 = (f32[4,64,128]{2,1,0:T(8,128)S(1)}, f32[4,64,128]{2,1,0:T(8,128)S(1)}, u32[]{:S(2)}, u32[]{:S(2)}) collective-permute-start(f32[4,64,128]{2,1,0:T(8,128)S(1)} %get-tuple-element.27.zo_ref), channel_id=1, source_target_pairs={{0,1},{1,2},{2,3},{3,4},{4,5},{5,6},{6,7},{8,9},{9,10},{10,11},{11... | collective-permute-start | bytes 393224 | tf_op jit(solution)/shard_map/ppermute | solution.py:575
  7.9 1.9 %collective-permute-start = (f32[4,64,128]{2,1,0:T(8,128)S(1)}, f32[4,64,128]{2,1,0:T(8,128)S(1)}, u32[]{:S(2)}, u32[]{:S(2)}) collective-permute-start(f32[4,64,128]{2,1,0:T(8,128)S(1)} %get-tuple-element.23), channel_id=1, source_target_pairs={{0,64},{64,128},{128,192},{192,256},{256,320},{320,384},{384,448},... | collective-permute-start | bytes 393224 | tf_op jit(solution)/shard_map/ppermute | solution.py:575
  9.8 3.5 %collective-permute-start.1 = (f32[4,64,128]{2,1,0:T(8,128)S(1)}, f32[4,64,128]{2,1,0:T(8,128)S(1)}, u32[]{:S(2)}, u32[]{:S(2)}) collective-permute-start(f32[4,64,128]{2,1,0:T(8,128)S(1)} %get-tuple-element.25), channel_id=1, source_target_pairs={{0,8},{8,16},{16,24},{24,32},{32,40},{40,48},{48,56},{1,9},{9,17},... | collective-permute-start | bytes 393224 | tf_op jit(solution)/shard_map/ppermute | solution.py:575
  13.3 0.0 copy-done.3
  13.3 0.0 copy-done
  13.4 0.8 %bend.1 = (f32[48,256]{1,0:T(8,128)S(1)}, f32[3,16,16,32]{3,2,1,0:T(8,128)S(1)}) custom-call(f32[3,8,8,16]{3,2,1,0:T(8,128)S(1)} %copy-done.3, f32[3,16,16,32]{3,2,1,0:T(8,128)S(1)} %copy-done), custom_call_target="tpu_custom_call" | custom-call | flops 4000000 | bytes 1000000 | tf_op jit(solution)/shard_map/bend/pallas_call | solution.py:207
  14.1 0.0 copy-done.6
  14.1 0.0 copy-done.8
  14.1 0.0 copy-start.1
  14.2 0.0 copy-start.2
  14.2 0.0 copy-start.4
  14.2 0.0 copy-start.5
  14.2 0.0 copy-start.7
  14.2 5.5 %interior.1 = (f32[12,48,128]{2,1,0:T(8,128)S(1)}, f32[6,24,128]{2,1,0:T(8,128)S(1)}) custom-call(f32[68,80,128]{2,1,0:T(8,128)S(1)} %get-tuple-element.19.s_ref, f32[64,64,128]{2,1,0:T(8,128)S(1)} %get-tuple-element.20.d_ref, bf16[48,128]{1,0:T(8,128)(2,1)S(1)} %copy-done.6, f32[384]{0:T(512)S(1)} %copy-done.8), custom_call_target="tpu_custom_call" | custom-call | flops 40000000 | bytes 4000000 | tf_op jit(solution)/shard_map/interior/pallas_call | solution.py:319
  19.7 0.0 collective-permute-done.2.zr_ref
  19.7 0.0 collective-permute-done.xr_ref
  19.7 0.0 collective-permute-done.1.yr_ref
  19.7 0.0 copy-done.1
  19.7 0.0 copy-done.2
  19.7 0.0 copy-done.4
  19.8 0.0 copy-done.5
  19.8 0.0 copy-done.7
  19.8 0.8 %finish.1 = (f32[8,48,128]{2,1,0:T(8,128)S(1)}, f32[48,256]{1,0:T(8,128)S(1)}) custom-call(f32[12,48,128]{2,1,0:T(8,128)S(1)} %get-tuple-element.21.af_ref, f32[6,24,128]{2,1,0:T(8,128)S(1)} %get-tuple-element.22.ac_ref, f32[4,64,128]{2,1,0:T(8,128)S(1)} %collective-permute-done.xr_ref, f32[4,64,128]{2,1,0:T(8,128)S(1)} %get-tuple-element.24.xo_ref, ...), custom_call_target="tpu_custom_call" | custom-call | tf_op jit(solution)/shard_map/finish/pallas_call | solution.py:416
  20.6 10.6 %all_to_all.15.got_ref = f32[8,48,128]{2,1,0:T(8,128)S(1)} all-to-all(f32[8,48,128]{2,1,0:T(8,128)S(1)} %get-tuple-element.29), channel_id=1, replica_groups=mesh['gx'=8,'gy'=8,'gz'=8] {'gx'}, dimensions={0} | all-to-all | bytes 393216 | tf_op jit(solution)/shard_map/all_to_all | solution.py:579
  31.2 0.1 xstage.1
  31.3 16.2 %all_to_all.16.got_ref = f32[8,48,128]{2,1,0:T(8,128)S(1)} all-to-all(f32[8,48,128]{2,1,0:T(8,128)S(1)} %get-tuple-element.31), channel_id=1, replica_groups=mesh['gx'=8,'gy'=8,'gz'=8] {'gy'}, dimensions={0} | all-to-all | bytes 393216 | tf_op jit(solution)/shard_map/all_to_all | solution.py:579
  47.5 0.2 ystage.1
  47.6 19.3 %all_to_all.17.got_ref = f32[8,56,128]{2,1,0:T(8,128)S(1)} all-to-all(f32[8,56,128]{2,1,0:T(8,128)S(1)} %get-tuple-element.33), channel_id=1, replica_groups=mesh['gx'=8,'gy'=8,'gz'=8] {'gz'}, dimensions={0} | all-to-all | bytes 458752 | tf_op jit(solution)/shard_map/all_to_all | solution.py:579
  67.0 1.5 %zstage.1 = (f32[3,8,8,16]{3,2,1,0:T(8,128)}, f32[3,16,16,32]{3,2,1,0:T(8,128)}) custom-call(f32[8,56,128]{2,1,0:T(8,128)S(1)} %all_to_all.17.got_ref, f32[48,256]{1,0:T(8,128)S(1)} %get-tuple-element.34.fine_ref, f32[3,16,16,32]{3,2,1,0:T(8,128)S(1)} %get-tuple-element.35.bk_ref), custom_call_target="tpu_custom_call" | custom-call | tf_op jit(solution)/shard_map/zstage/pallas_call | solution.py:561
Async XLA Ops:
  0.6 13.5 %copy-start.6 = (bf16[48,128]{1,0:T(8,128)(2,1)S(1)}, bf16[48,128]{1,0:T(8,128)(2,1)}, u32[]{:S(2)}) copy-start(bf16[48,128]{1,0:T(8,128)(2,1)} %constant.14.clone.left_ref) | copy-start | bytes 36868
  0.6 13.5 %copy-start.8 = (f32[384]{0:T(512)S(1)}, f32[384]{0:T(512)}, u32[]{:S(2)}) copy-start(f32[384]{0:T(512)} %constant.15.clone.cx_ref) | copy-start | bytes 4612
  0.7 12.7 %copy-start.3 = (f32[3,8,8,16]{3,2,1,0:T(8,128)S(1)}, f32[3,8,8,16]{3,2,1,0:T(8,128)}, u32[]{:S(2)}) copy-start(f32[3,8,8,16]{3,2,1,0:T(8,128)} %c_ref.1) | copy-start | bytes 36868
  0.7 12.7 %copy-start = (f32[3,16,16,32]{3,2,1,0:T(8,128)S(1)}, f32[3,16,16,32]{3,2,1,0:T(8,128)}, u32[]{:S(2)}) copy-start(f32[3,16,16,32]{3,2,1,0:T(8,128)} %k_ref.1) | copy-start | bytes 294916
  3.6 16.1 %collective-permute-start.2 = (f32[4,64,128]{2,1,0:T(8,128)S(1)}, f32[4,64,128]{2,1,0:T(8,128)S(1)}, u32[]{:S(2)}, u32[]{:S(2)}) collective-permute-start(f32[4,64,128]{2,1,0:T(8,128)S(1)} %get-tuple-element.27.zo_ref), channel_id=1, source_target_pairs={{0,1},{1,2},{2,3},{3,4},{4,5},{5,6},{6,7},{8,9},{9,10},{10,11},{11... | collective-permute-start | bytes 393224 | tf_op jit(solution)/shard_map/ppermute | solution.py:575
  7.9 11.8 %collective-permute-start = (f32[4,64,128]{2,1,0:T(8,128)S(1)}, f32[4,64,128]{2,1,0:T(8,128)S(1)}, u32[]{:S(2)}, u32[]{:S(2)}) collective-permute-start(f32[4,64,128]{2,1,0:T(8,128)S(1)} %get-tuple-element.23), channel_id=1, source_target_pairs={{0,64},{64,128},{128,192},{192,256},{256,320},{320,384},{384,448},... | collective-permute-start | bytes 393224 | tf_op jit(solution)/shard_map/ppermute | solution.py:575
  9.8 9.9 %collective-permute-start.1 = (f32[4,64,128]{2,1,0:T(8,128)S(1)}, f32[4,64,128]{2,1,0:T(8,128)S(1)}, u32[]{:S(2)}, u32[]{:S(2)}) collective-permute-start(f32[4,64,128]{2,1,0:T(8,128)S(1)} %get-tuple-element.25), channel_id=1, source_target_pairs={{0,8},{8,16},{16,24},{24,32},{32,40},{40,48},{48,56},{1,9},{9,17},... | collective-permute-start | bytes 393224 | tf_op jit(solution)/shard_map/ppermute | solution.py:575
  14.1 5.6 %copy-start.1 = (bf16[2,128,384]{2,1,0:T(8,128)(2,1)S(1)}, bf16[2,128,384]{2,1,0:T(8,128)(2,1)}, u32[]{:S(2)}) copy-start(bf16[2,128,384]{2,1,0:T(8,128)(2,1)} %constant.19.clone.mh_ref) | copy-start | bytes 589828
  14.2 5.6 %copy-start.2 = (bf16[2,128,384]{2,1,0:T(8,128)(2,1)S(1)}, bf16[2,128,384]{2,1,0:T(8,128)(2,1)}, u32[]{:S(2)}) copy-start(bf16[2,128,384]{2,1,0:T(8,128)(2,1)} %constant.20.clone.ml_ref) | copy-start | bytes 589828
  14.2 5.6 %copy-start.4 = (bf16[2,128,128]{2,1,0:T(8,128)(2,1)S(1)}, bf16[2,128,128]{2,1,0:T(8,128)(2,1)}, u32[]{:S(2)}) copy-start(bf16[2,128,128]{2,1,0:T(8,128)(2,1)} %constant.17.clone.wzh_ref) | copy-start | bytes 196612
  14.2 5.6 %copy-start.5 = (bf16[2,128,128]{2,1,0:T(8,128)(2,1)S(1)}, bf16[2,128,128]{2,1,0:T(8,128)(2,1)}, u32[]{:S(2)}) copy-start(bf16[2,128,128]{2,1,0:T(8,128)(2,1)} %constant.18.clone.wzl_ref) | copy-start | bytes 196612
  14.2 5.6 %copy-start.7 = (f32[8,8,128]{2,1,0:T(8,128)S(1)}, f32[8,8,128]{2,1,0:T(8,128)}, u32[]{:S(2)}) copy-start(f32[8,8,128]{2,1,0:T(8,128)} %constant.16.clone.wc_ref) | copy-start | bytes 98308

commit v2 on v1

--- a/solution.py
+++ b/solution.py
@@ -69,11 +69,11 @@
     return [pl.BlockSpec(memory_space=VMEM)] * n
 
 
-STEP = 16
+STEP = 8
 PARTS = 64 // STEP
 
 
-def faces_kernel(w_hbm, f_hbm, xf_ref, xo_ref, yf_ref, yo_ref, zf_ref, s_ref, d_ref, w_ref, f_ref, sem):
+def faces_kernel(w_hbm, f_hbm, xf_ref, xo_ref, yf_ref, yo_ref, zf_ref, s_ref, t_ref, d_ref, w_ref, f_ref, sem):
     def copies(g):
         part = pl.ds(g * STEP, STEP)
         return [
@@ -85,10 +85,11 @@
         for copy in copies(g):
             copy.start()
     lane = lanes((64, 128))
-    s_ref[:, 0:8, :] = jnp.zeros((68, 8, 128), f32)
-    s_ref[:, 72:80, :] = jnp.zeros((68, 8, 128), f32)
-    for x in (0, 1, 66, 67):
-        s_ref[x, 8:72, :] = jnp.zeros((64, 128), f32)
+    for ref in (s_ref, t_ref):
+        ref[:, 0:8, :] = jnp.zeros((68, 8, 128), f32)
+        ref[:, 72:80, :] = jnp.zeros((68, 8, 128), f32)
+        for x in (0, 1, 66, 67):
+            ref[x, 8:72, :] = jnp.zeros((64, 128), f32)
 
     def part(g, carry):
         for copy in copies(g):
@@ -102,6 +103,7 @@
             s = w + f
             d = w - f
             s_ref[x + 2, 8:72, :] = s
+            t_ref[x + 2, 8:72, :] = 8.0 * s
             d_ref[x] = d
             row = pl.ds(x, 1)
             for j in range(2):
@@ -112,18 +114,10 @@
             here = (lane >= 4 * i) & (lane < 4 * i + 4)
             packed_s = jnp.where(here, rolled(s, 4 * i + 2), packed_s)
             packed_d = jnp.where(here, rolled(d, 4 * i + 2), packed_d)
-        half = g // 2
-
-        @pl.when(g % 2 == 0)
-        def _():
-            zf_ref[half] = packed_s
-            zf_ref[2 + half] = packed_d
-
-        @pl.when(g % 2 == 1)
-        def _():
-            zf_ref[half] = jnp.where(lane < 64, zf_ref[half], rolled(packed_s, 64))
-            zf_ref[2 + half] = jnp.where(lane < 64, zf_ref[2 + half], rolled(packed_d, 64))
-
+        half, quarter = g // 4, g % 4
+        here = lane // 32 == quarter
+        for i, packed in ((half, packed_s), (2 + half, packed_d)):
+            zf_ref[i] = jnp.where(here, pltpu.roll(packed, 32 * quarter, 1), zf_ref[i])
         return carry
 
     lax.fori_loop(0, PARTS, part, 0)
@@ -135,11 +129,11 @@
 
 
 def faces(w, f):
-    shapes = [(4, 64, 128)] * 5 + [(68, 80, 128), (64, 64, 128)]
+    shapes = [(4, 64, 128)] * 5 + [(68, 80, 128)] * 2 + [(64, 64, 128)]
     return pl.pallas_call(
         faces_kernel,
         in_specs=[pl.BlockSpec(memory_space=pltpu.HBM)] * 2,
-        out_specs=whole(7),
+        out_specs=whole(8),
         out_shape=[jax.ShapeDtypeStruct(s, f32) for s in shapes],
         scratch_shapes=[
             VMEM((64, 64, 128), f32),
@@ -151,7 +145,7 @@
     )(*(pltpu.with_memory_space_constraint(v, pltpu.HBM) for v in (w, f)))
 
 
-def bend_kernel(sizes, c_ref, k_ref, bf_ref, bk_ref, u_ref, a_ref, b_ref):
+def bend_kernel(sizes, c_ref, k_ref, bf_ref, bk_ref, u_ref, k2_ref):
     nx, ny, nz = sizes
     ix, iy, iz = (lax.axis_index(n) for n in ("gx", "gy", "gz"))
     u_ref[...] = jnp.zeros_like(u_ref)
@@ -166,53 +160,50 @@
     gq = row - 2 + 8 * iy
     inside = (gp >= 0) & (gp < 8 * nx) & (gq >= 0) & (gq < 8 * ny) & (gr >= 0) & (gr < 16 * nz)
 
-    def around(u):
-        total = pltpu.roll(u, 1, 0) + pltpu.roll(u, 47, 0)
-        for shift in (1, 255, 20, 236):
-            total = total + pltpu.roll(u, shift, 1)
+    def around(u, step):
+        total = pltpu.roll(u, 1, 0) + pltpu.roll(u, u.shape[0] - 1, 0)
+        for shift in (1, -1, step, -step):
+            total = total + rolled(u, shift)
         return total - 6.0 * u
 
-    u = around(u_ref[...])
-    u = around(jnp.where(inside, u, 0.0)) * BEND
+    u = around(u_ref[...], 20)
+    u = around(jnp.where(inside, u, 0.0), 20) * BEND
     keep = lanes((48, 128)) < 120
     bf_ref[:, 0:128] = jnp.where(keep, u[:, 0:128], 0.0)
     bf_ref[:, 128:256] = jnp.where(keep, pltpu.roll(u, 136, 1)[:, 0:128], 0.0)
 
     kx, ky, kz = 2 * nx, 2 * ny, 4 * nz
-    a_ref[...] = jnp.zeros_like(a_ref)
-    b_ref[...] = jnp.zeros_like(b_ref)
+    k2_ref[...] = jnp.zeros_like(k2_ref)
+    parts = []
     for a in range(3):
-        for p in range(kx):
-            a_ref[a, p + 1, 8 : 8 + ky, 0:kz] = k_ref[a, p]
-    grid = lanes((ky, 128)) < kz
-
-    def star(ref, a, p):
-        mid = ref[a, p + 1, 8 : 8 + ky, :]
-        total = ref[a, p, 8 : 8 + ky, :] + ref[a, p + 2, 8 : 8 + ky, :]
-        total = total + ref[a, p + 1, 7 : 7 + ky, :] + ref[a, p + 1, 9 : 9 + ky, :]
-        total = total + rolled(mid, 1) + rolled(mid, 127)
-        return total - 6.0 * mid
-
-    for a in range(3):
-        for p in range(kx):
-            b_ref[a, p + 1, 8 : 8 + ky, :] = jnp.where(grid, star(a_ref, a, p), 0.0)
-    for a in range(3):
-        for p in range(kx):
-            bk_ref[a, p] = (star(b_ref, a, p) * BEND)[:, 0:kz]
+        total = None
+        for p in range(6):
+            i = 6 * a + p
+            k2_ref[i, 0:ky, 0:kz] = k_ref[a, jnp.clip(2 * ix - 2 + p, 0, kx - 1)]
+            tile = pltpu.roll(k2_ref[i], (18 - 2 * iy) % 16, 0)[0:8]
+            tile = pltpu.roll(tile, (130 - 4 * iz + 8 * p) % 128, 1)
+            total = tile if p == 0 else jnp.where(lanes((8, 128)) // 8 == p, tile, total)
+        parts.append(total)
+    lane = lanes((24, 128))
+    row = rows_of((24, 128)) % 8
+    gp, gq, gr = 2 * ix - 2 + lane // 8, 2 * iy - 2 + row, 4 * iz - 2 + lane % 8
+    inside = (gp >= 0) & (gp < kx) & (gq >= 0) & (gq < ky) & (gr >= 0) & (gr < kz) & (lane < 48)
+    u = jnp.where(inside, jnp.concatenate(parts, 0), 0.0)
+    u = around(jnp.where(inside, around(u, 8), 0.0), 8) * BEND
+    own = (lane // 16 == 1) & (row // 2 == 1) & ((lane % 8 + 2) // 4 == 1)
+    bk_ref[...] = rolled(jnp.where(own, u, 0.0), 80)
 
 
 def bend(sizes, control, coarse):
-    nx, ny, nz = sizes
-    grid = (3, 2 * nx + 2, 2 * ny + 16, 128)
     return pl.pallas_call(
         functools.partial(bend_kernel, sizes),
         in_specs=whole(2),
         out_specs=whole(2),
         out_shape=[
             jax.ShapeDtypeStruct((48, 256), f32),
-            jax.ShapeDtypeStruct(coarse.shape, f32),
-        ],
-        scratch_shapes=[VMEM((48, 256), f32), VMEM(grid, f32), VMEM(grid, f32)],
+            jax.ShapeDtypeStruct((24, 128), f32),
+        ],
+        scratch_shapes=[VMEM((48, 256), f32), VMEM((18, 16, 128), f32)],
         cost_estimate=pl.CostEstimate(flops=4000000, bytes_accessed=1000000, transcendentals=0),
         compiler_params=within(8),
         name="bend",
@@ -240,13 +231,15 @@
     wz[0, :, 0:20] = weights(np.arange(128), 20, SPF) * fine_scale
     wz[1, :, 0:8] = weights(np.arange(128), 8, SPC) * coarse_scale
     wz_high, wz_low = halves(wz)
-    m = np.zeros((2, 128, 384))
+    m = np.zeros((4, 128, 384))
     fx, cx = weights(own, 12, SPF), weights(own, 6, SPC)
     fz = weights(cross, 20, SPF) * fine_scale
     cz = weights(cross, 8, SPC) * coarse_scale
+    fz = np.concatenate([fz, weights(np.arange(126, 128), 20, SPF) * fine_scale])
+    cz = np.concatenate([cz, weights(np.arange(126, 128), 8, SPC) * coarse_scale])
     for x in range(64):
-        for j in range(4):
-            line = m[x // 32, 4 * (x % 32) + j]
+        for j in range(6):
+            line = m[x // 32 + 2 * (j // 4), 4 * (x % 32) + j % 4]
             for p in range(12):
                 at = 128 * (p // 6) + 20 * (p % 6)
                 line[at : at + 20] = fx[x, p] * fz[j]
@@ -254,8 +247,7 @@
                 at = 256 + 80 + 8 * p
                 line[at : at + 8] = cx[x, p] * cz[j]
     m_high, m_low = halves(m)
-    coarse_x = weights(own, 6, SPC).astype(np.float32).reshape(-1)
-    return left, wc, wz_high, wz_low, m_high, m_low, coarse_x
+    return left, wc, wz_high, wz_low, m_high, m_low
 
 
 def along(left, force):
@@ -264,61 +256,57 @@
     return both[0:24] + both[24:48]
 
 
-def interior_kernel(s_ref, d_ref, left_ref, cx_ref, af_ref, ac_ref, tf_ref, tc_ref):
+def interior_kernel(s_ref, t_ref, d_ref, left_ref, af_ref, ac_ref, tf_ref, tc_ref):
     fx = weights(np.arange(8), 5, SPF)
+    cx = weights(np.arange(64), 6, SPC)
     left = left_ref[...]
-    lane = lanes((64, 128))
-
-    def layer(x, carry):
-        s = s_ref[x + 2, 8:72, :]
+
+    def force(x):
         d = d_ref[x]
-        below, above = s_ref[x + 1, 8:72, :], s_ref[x + 3, 8:72, :]
-        f0 = (s_ref[x, 8:72, :] - s_ref[x + 4, 8:72, :]) + 8.0 * (above - below)
-        f1 = (s_ref[x + 2, 6:70, :] - s_ref[x + 2, 10:74, :]) + 8.0 * (
-            s_ref[x + 2, 9:73, :] - s_ref[x + 2, 7:71, :]
-        )
-        f2 = jnp.where(lane >= 2, rolled(s, 2), 0.0) - jnp.where(lane < 126, rolled(s, 126), 0.0)
-        f2 = f2 + 8.0 * (
-            jnp.where(lane < 127, rolled(s, 127), 0.0) - jnp.where(lane >= 1, rolled(s, 1), 0.0)
-        )
-        t = along(left, jnp.concatenate([f0 * d, f1 * d, f2 * d], 1))
-        for a in range(3):
-            cols = slice(128 * a, 128 * a + 128)
-            tf_ref[x, 16 * a : 16 * a + 16, :] = t[0:16, cols]
-            tc_ref[x, 8 * a : 8 * a + 8, :] = t[16:24, cols]
-        return carry
-
-    lax.fori_loop(0, 64, layer, 0, unroll=8)
+        f0 = (s_ref[x, 8:72, :] - s_ref[x + 4, 8:72, :]) + (t_ref[x + 3, 8:72, :] - t_ref[x + 1, 8:72, :])
+        s, t = s_ref.at[x + 2], t_ref.at[x + 2]
+        f1 = (s[6:70, :] - s[10:74, :]) + (t[9:73, :] - t[7:71, :])
+        s, t = s[8:72, :], t[8:72, :]
+        f2 = (rolled(s, 2) - rolled(s, 126)) + (rolled(t, 127) - rolled(t, 1))
+        return [f0 * d, f1 * d, f2 * d]
+
+    def layers(b):
+        for i in range(0, 8, 2):
+            section = along(left, jnp.concatenate(force(8 * b + i) + force(8 * b + i + 1), 1))
+            for k in range(6):
+                at, a = 8 * b + i + k // 3, k % 3
+                cols = slice(128 * k, 128 * k + 128)
+                tf_ref[at, 16 * a : 16 * a + 16, :] = section[0:16, cols]
+                tc_ref[at, 8 * a : 8 * a + 8, :] = section[16:24, cols]
+
+    def block(b):
+        for k in range(5):
+            total = af_ref[b + k]
+            for r in range(8):
+                weight = float(fx[r, k])
+                if weight != 0.0:
+                    total = total + weight * tf_ref[8 * b + r]
+            af_ref[b + k] = total
+        for k in range((b + 2) // 4, (b + 2) // 4 + 4):
+            total = ac_ref[k]
+            for r in range(8):
+                total = total + float(cx[8 * b + r, k]) * tc_ref[8 * b + r]
+            ac_ref[k] = total
 
     af_ref[...] = jnp.zeros_like(af_ref)
     ac_ref[...] = jnp.zeros_like(ac_ref)
-
-    def block(b, carry):
-        for k in range(5):
-            total = None
-            for r in range(8):
-                weight = float(fx[r, k])
-                if weight == 0.0:
-                    continue
-                term = weight * tf_ref[8 * b + r]
-                total = term if total is None else total + term
-            af_ref[b + k] += total
-        for k in range(6):
-            total = None
-            for r in range(8):
-                term = cx_ref[(8 * b + r) * 6 + k] * tc_ref[8 * b + r]
-                total = term if total is None else total + term
-            ac_ref[k] += total
-        return carry
-
-    lax.fori_loop(0, 8, block, 0)
-
-
-def interior(s, d):
-    left, *_, coarse_x = tables()
+    for b in range(8):
+        layers(b)
+        if b > 0:
+            block(b - 1)
+    block(7)
+
+
+def interior(s, s8, d):
+    left = tables()[0]
     return pl.pallas_call(
         interior_kernel,
-        in_specs=whole(3) + [pl.BlockSpec(memory_space=pltpu.SMEM)],
+        in_specs=whole(4),
         out_specs=whole(2),
         out_shape=[
             jax.ShapeDtypeStruct((12, 48, 128), f32),
@@ -328,7 +316,7 @@
         cost_estimate=pl.CostEstimate(flops=40000000, bytes_accessed=4000000, transcendentals=0),
         compiler_params=within(16),
         name="interior",
-    )(s, d, jnp.asarray(left), jnp.asarray(coarse_x))
+    )(s, s8, d, jnp.asarray(left))
 
 
 def crossing(first, second):
@@ -338,7 +326,7 @@
 
 
 def finish_kernel(
-    af_ref, ac_ref, xr_ref, xo_ref, yr_ref, yo_ref, zr_ref, zo_ref, bf_ref, left_ref, wc_ref, wzh_ref, wzl_ref, mh_ref, ml_ref,
+    af_ref, ac_ref, xr_ref, xo_ref, yr_ref, yo_ref, zr_ref, zo_ref, bf_ref, bk_ref, left_ref, wc_ref, wzh_ref, wzl_ref, mh_ref, ml_ref,
     chunk_ref, fine_ref, sf_ref, sc_ref,
 ):
     n = chunk_ref.shape[0]
@@ -380,20 +368,22 @@
         for i in range(1, 6):
             total = total + rolled(zf[48 * (6 * h + i) : 48 * (6 * h + i) + 48], 20 * i)
         fine.append(total + bf_ref[:, 128 * h : 128 * h + 128])
-    coarse = rolled(zc[0:24], 80)
+    coarse = bk_ref[...] + rolled(zc[0:24], 80)
     for p in range(1, 6):
         coarse = coarse + rolled(zc[24 * p : 24 * p + 24], 80 + 8 * p)
 
     j = lane % 4
     extra = None
     for h in range(2):
-        s = jnp.where(j < 2, zr_ref[h], zo_ref[h])
+        s = jnp.where(j < 2, zr_ref[h] - zo_ref[h], zo_ref[h])
         d = jnp.where(j < 2, zr_ref[2 + h], zo_ref[2 + h])
         slope = jnp.where(j >= 2, rolled(s, 2), 0.0) - jnp.where(j < 2, rolled(s, 126), 0.0)
         slope = slope + 8.0 * (
             jnp.where(j == 1, rolled(s, 127), 0.0) - jnp.where(j == 2, rolled(s, 1), 0.0)
         )
-        part = mm3(along(left, slope * d), mh_ref[h], ml_ref[h])
+        wrapped = jnp.where(j < 2, -slope * zo_ref[2 + h], 0.0)
+        part = along(left, jnp.concatenate([slope * d, wrapped], 1))
+        part = mm3(part[:, 0:128], mh_ref[h], ml_ref[h]) + mm3(part[:, 128:256], mh_ref[2 + h], ml_ref[2 + h])
         extra = part if extra is None else extra + part
 
     zero8 = jnp.zeros((8, 128), f32)
@@ -412,10 +402,10 @@
 
 
 def finish(n, *values):
-    constants = tables()[:-1]
+    constants = tables()
     return pl.pallas_call(
         finish_kernel,
-        in_specs=whole(15),
+        in_specs=whole(16),
         out_specs=whole(2),
         out_shape=[
             jax.ShapeDtypeStruct((n, 48, 128), f32),
@@ -521,7 +511,7 @@
     )(got, fine)
 
 
-def z_kernel(nx, ny, got_ref, fine_ref, bk_ref, out_fine_ref, out_coarse_ref):
+def z_kernel(nx, ny, got_ref, fine_ref, out_fine_ref, out_coarse_ref):
     n = got_ref.shape[0]
     low, has_low, high, has_high = sides(got_ref, "gz")
     low = jnp.where(has_low, low[48:56], 0.0)
@@ -539,36 +529,39 @@
     lane = lanes((48, 128))
     k = lane % 8
     parts = [got_ref[m, 0:48, :] for m in range(n)]
-    sums = []
-    for m in range(n):
-        total = parts[m]
+    tiles = []
+    for m in range(0, n, 2):
+        total = jnp.where(k < 6, rolled(parts[m], -2), 0.0) + jnp.where(k >= 2, rolled(parts[m + 1], 2), 0.0)
         if m > 0:
-            total = total + jnp.where(k < 4, rolled(parts[m - 1], -4), 0.0)
-        if m < n - 1:
-            total = total + jnp.where(k >= 4, rolled(parts[m + 1], 4), 0.0)
-        sums.append(jnp.where((k >= 2) & (k < 6), total, 0.0))
-    tiles = [rolled(sums[2 * m], -2) + rolled(sums[2 * m + 1], 2) for m in range(n // 2)]
-    for p in range(2 * nx):
-        total = None
-        for m in range(n // 2):
-            moved = rolled(tiles[m], 8 * m - 8 * p)
-            total = moved if total is None else jnp.where(lane >= 8 * m, moved, total)
-        for a in range(3):
-            out_coarse_ref[a, p] = total[16 * a : 16 * a + 2 * ny, 0 : 4 * n] + bk_ref[a, p]
-
-
-def z_stage(nx, ny, got, fine, bent):
+            total = total + jnp.where(k < 2, rolled(parts[m - 1], -6), 0.0)
+        if m + 2 < n:
+            total = total + jnp.where(k >= 6, rolled(parts[m + 2], 6), 0.0)
+        tiles.append(total)
+    per = len(tiles)
+    slot = lane // 8 % per
+    for h in range(per):
+        total = rolled(tiles[0], -8 * h)
+        for m in range(1, per):
+            total = jnp.where(slot == m, rolled(tiles[m], 8 * (m - h)), total)
+        for g in range(2 * nx // per):
+            points = rolled(total, -8 * per * g)
+            for a in range(3):
+                out_coarse_ref[a, per * g + h] = points[16 * a : 16 * a + 2 * ny, 0 : 4 * n]
+
+
+def z_stage(sizes, got, fine):
+    nx, ny, nz = sizes
     return pl.pallas_call(
         functools.partial(z_kernel, nx, ny),
-        in_specs=whole(3),
+        in_specs=whole(2),
         out_specs=whole(2),
         out_shape=[
             jax.ShapeDtypeStruct((3, 8, 8, 16), f32),
-            jax.ShapeDtypeStruct(bent.shape, f32),
+            jax.ShapeDtypeStruct((3, 2 * nx, 2 * ny, 4 * nz), f32),
         ],
         compiler_params=within(6),
         name="zstage",
-    )(got, fine, bent)
+    )(got, fine)
 
 
 def shifted_up(values, axis):
@@ -581,16 +574,16 @@
 
 def per_device(warped_image, fixed_image, fine_control, coarse_control):
     sizes = tuple(lax.axis_size(n) for n in ("gx", "gy", "gz"))
-    xf, xo, yf, yo, zf, s, d = faces(warped_image, fixed_image)
+    xf, xo, yf, yo, zf, s, s8, d = faces(warped_image, fixed_image)
     zr = shifted_up(zf, "gz")
     yr = shifted_up(yf, "gy")
     xr = shifted_up(xf, "gx")
     bent_fine, bent_coarse = bend(sizes, fine_control, coarse_control)
-    fine, coarse = interior(s, d)
-    chunk, fine = finish(sizes[0], fine, coarse, xr, xo, yr, yo, zr, zf, bent_fine)
+    fine, coarse = interior(s, s8, d)
+    chunk, fine = finish(sizes[0], fine, coarse, xr, xo, yr, yo, zr, zf, bent_fine, bent_coarse)
     chunk, fine = x_stage(sizes[1], exchanged(chunk, "gx"), fine)
     chunk, fine = y_stage(sizes[2], exchanged(chunk, "gy"), fine)
-    return tuple(z_stage(sizes[0], sizes[1], exchanged(chunk, "gz"), fine, bent_coarse))
+    return tuple(z_stage(sizes, exchanged(chunk, "gz"), fine))
 
 
 def solution(mesh):

time: 68.7 us -> 68.9 us (level)
  blocking collectives: 46.1 us -> 48.5 us
  Pallas kernels: 11.7 us -> 9.47 us
    pallas_call x3, Pallas kernels: 7.79 us -> 5.24 us  [the longest x1 2.94 us: interior(): pl.pallas_call(interior_kernel, in_specs=whole(4), out_specs=whole(2), ou...]
    all_to_all x3, blocking collectives: 46.1 us -> 48.5 us  [exchanged(): return lax.all_to_all(chunks, axis, split_axis=0, concat_axis=0, tiled=True)]
  transfers between devices with their start and end apart: 3 -> 3, of which waited for: 0 -> 0; matrix products, arithmetic and copies ran while one was open for 0% -> 0% of each run, Pallas kernels for 9% -> 5%
where the time goes in v2:
time: 68.9 us; the launch traced here: 68.6 us
  blocking collectives  48.5 us (70%)
  starting transfers between devices  9.69 us (14%)
  Pallas kernels  9.47 us (14%)
  between operations  0.83 us (1%)
    all_to_all x3, blocking collectives, exchanged(): return lax.all_to_all(chunks, axis, split_axis=0, concat_axis=0, tiled=True)  48.5 us
    ppermute x3, starting transfers between devices, shifted_up(): lax.ppermute(values, axis, [(i, i + 1) for i in range(lax.axis_size(axis)...  9.69 us
    pallas_call x1, Pallas kernels, faces(): pl.pallas_call(faces_kernel, in_specs=[pl.BlockSpec(memory_space=pltpu.HB...  3.53 us
    pallas_call x1, Pallas kernels, interior(): pl.pallas_call(interior_kernel, in_specs=whole(4), out_specs=whole(2), ou...  2.94 us
  transfers between devices with their start and end apart: 3, of which 0 were waited for; matrix products, arithmetic and copies ran while one was open for 0% of the time, Pallas kernels for 5%

profile of v2, /device:TPU:2, one launch (start us, length us, event | category | flops | bytes accessed | tf_op | source)
XLA Modules:
  0.0 68.6 jit_solution(6285777656813146480)
XLA Ops:
  0.6 0.0 copy-start.6
  0.6 0.0 copy-start.3
  0.7 0.0 copy-start
  0.7 3.5 %faces.1 = (f32[4,64,128]{2,1,0:T(8,128)S(1)}, f32[4,64,128]{2,1,0:T(8,128)S(1)}, f32[4,64,128]{2,1,0:T(8,128)S(1)}, f32[4,64,128]{2,1,0:T(8,128)S(1)}, f32[4,64...) custom-call(f32[64,64,128]{2,1,0:T(8,128)} %w_hbm.1, ...), custom_call_target="tpu_custom_call" | custom-call | tf_op jit(solution)/shard_map/faces/pallas_call | solution.py:133
  4.2 4.3 %collective-permute-start.2 = (f32[4,64,128]{2,1,0:T(8,128)S(1)}, f32[4,64,128]{2,1,0:T(8,128)S(1)}, u32[]{:S(2)}, u32[]{:S(2)}) collective-permute-start(f32[4,64,128]{2,1,0:T(8,128)S(1)} %get-tuple-element.29.zo_ref), channel_id=1, source_target_pairs={{0,1},{1,2},{2,3},{3,4},{4,5},{5,6},{6,7},{8,9},{9,10},{10,11},{11... | collective-permute-start | bytes 393224 | tf_op jit(solution)/shard_map/ppermute | solution.py:568
  8.5 1.9 %collective-permute-start = (f32[4,64,128]{2,1,0:T(8,128)S(1)}, f32[4,64,128]{2,1,0:T(8,128)S(1)}, u32[]{:S(2)}, u32[]{:S(2)}) collective-permute-start(f32[4,64,128]{2,1,0:T(8,128)S(1)} %get-tuple-element.25), channel_id=1, source_target_pairs={{0,64},{64,128},{128,192},{192,256},{256,320},{320,384},{384,448},... | collective-permute-start | bytes 393224 | tf_op jit(solution)/shard_map/ppermute | solution.py:568
  10.4 3.5 %collective-permute-start.1 = (f32[4,64,128]{2,1,0:T(8,128)S(1)}, f32[4,64,128]{2,1,0:T(8,128)S(1)}, u32[]{:S(2)}, u32[]{:S(2)}) collective-permute-start(f32[4,64,128]{2,1,0:T(8,128)S(1)} %get-tuple-element.27), channel_id=1, source_target_pairs={{0,8},{8,16},{16,24},{24,32},{32,40},{40,48},{48,56},{1,9},{9,17},... | collective-permute-start | bytes 393224 | tf_op jit(solution)/shard_map/ppermute | solution.py:568
  13.9 0.0 copy-done.3
  13.9 0.0 copy-done
  13.9 0.4 bend.1
  14.4 0.0 copy-done.6
  14.4 0.0 copy-start.1
  14.4 0.0 copy-start.2
  14.4 0.0 copy-start.4
  14.4 0.0 copy-start.5
  14.4 0.0 copy-start.7
  14.5 2.9 %interior.1 = (f32[12,48,128]{2,1,0:T(8,128)S(1)}, f32[6,24,128]{2,1,0:T(8,128)S(1)}) custom-call(f32[68,80,128]{2,1,0:T(8,128)S(1)} %get-tuple-element.20.s_ref, f32[68,80,128]{2,1,0:T(8,128)S(1)} %get-tuple-element.21.t_ref, f32[64,64,128]{2,1,0:T(8,128)S(1)} %get-tuple-element.22.d_ref, bf16[48,128]{1,0:T(8,128)(2,1)S(1)} %copy-done.6), custom_call_target="tpu_custom_call" | custom-call | flops 40000000 | bytes 4000000 | tf_op jit(solution)/shard_map/interior/pallas_call | solution.py:307
  17.4 0.0 collective-permute-done.2.zr_ref
  17.4 0.0 collective-permute-done.xr_ref
  17.4 0.0 collective-permute-done.1.yr_ref
  17.4 0.0 copy-done.1
  17.4 0.0 copy-done.2
  17.5 0.0 copy-done.4
  17.5 0.0 copy-done.5
  17.5 0.0 copy-done.7
  17.5 0.9 %finish.1 = (f32[8,48,128]{2,1,0:T(8,128)S(1)}, f32[48,256]{1,0:T(8,128)S(1)}) custom-call(f32[12,48,128]{2,1,0:T(8,128)S(1)} %get-tuple-element.23.af_ref, f32[6,24,128]{2,1,0:T(8,128)S(1)} %get-tuple-element.24.ac_ref, f32[4,64,128]{2,1,0:T(8,128)S(1)} %collective-permute-done.xr_ref, f32[4,64,128]{2,1,0:T(8,128)S(1)} %get-tuple-element.26.xo_ref, ...), custom_call_target="tpu_custom_call" | custom-call | tf_op jit(solution)/shard_map/finish/pallas_call | solution.py:406
  18.4 10.6 %all_to_all.15.got_ref = f32[8,48,128]{2,1,0:T(8,128)S(1)} all-to-all(f32[8,48,128]{2,1,0:T(8,128)S(1)} %get-tuple-element.32), channel_id=1, replica_groups=mesh['gx'=8,'gy'=8,'gz'=8] {'gx'}, dimensions={0} | all-to-all | bytes 393216 | tf_op jit(solution)/shard_map/all_to_all | solution.py:572
  29.0 0.1 xstage.1
  29.1 18.6 %all_to_all.16.got_ref = f32[8,48,128]{2,1,0:T(8,128)S(1)} all-to-all(f32[8,48,128]{2,1,0:T(8,128)S(1)} %get-tuple-element.34), channel_id=1, replica_groups=mesh['gx'=8,'gy'=8,'gz'=8] {'gy'}, dimensions={0} | all-to-all | bytes 393216 | tf_op jit(solution)/shard_map/all_to_all | solution.py:572
  47.7 0.2 ystage.1
  47.9 19.3 %all_to_all.17.got_ref = f32[8,56,128]{2,1,0:T(8,128)S(1)} all-to-all(f32[8,56,128]{2,1,0:T(8,128)S(1)} %get-tuple-element.36), channel_id=1, replica_groups=mesh['gx'=8,'gy'=8,'gz'=8] {'gz'}, dimensions={0} | all-to-all | bytes 458752 | tf_op jit(solution)/shard_map/all_to_all | solution.py:572
  67.2 1.4 %zstage.1 = (f32[3,8,8,16]{3,2,1,0:T(8,128)}, f32[3,16,16,32]{3,2,1,0:T(8,128)}) custom-call(f32[8,56,128]{2,1,0:T(8,128)S(1)} %all_to_all.17.got_ref, f32[48,256]{1,0:T(8,128)S(1)} %get-tuple-element.37.fine_ref), custom_call_target="tpu_custom_call" | custom-call | tf_op jit(solution)/shard_map/zstage/pallas_call | solution.py:554
Async XLA Ops:
  0.6 13.8 %copy-start.6 = (bf16[48,128]{1,0:T(8,128)(2,1)S(1)}, bf16[48,128]{1,0:T(8,128)(2,1)}, u32[]{:S(2)}) copy-start(bf16[48,128]{1,0:T(8,128)(2,1)} %constant.12.clone.left_ref) | copy-start | bytes 36868
  0.6 13.3 %copy-start.3 = (f32[3,8,8,16]{3,2,1,0:T(8,128)S(1)}, f32[3,8,8,16]{3,2,1,0:T(8,128)}, u32[]{:S(2)}) copy-start(f32[3,8,8,16]{3,2,1,0:T(8,128)} %c_ref.1) | copy-start | bytes 36868
  0.7 13.3 %copy-start = (f32[3,16,16,32]{3,2,1,0:T(8,128)S(1)}, f32[3,16,16,32]{3,2,1,0:T(8,128)}, u32[]{:S(2)}) copy-start(f32[3,16,16,32]{3,2,1,0:T(8,128)} %k_ref.1) | copy-start | bytes 294916
  4.2 13.2 %collective-permute-start.2 = (f32[4,64,128]{2,1,0:T(8,128)S(1)}, f32[4,64,128]{2,1,0:T(8,128)S(1)}, u32[]{:S(2)}, u32[]{:S(2)}) collective-permute-start(f32[4,64,128]{2,1,0:T(8,128)S(1)} %get-tuple-element.29.zo_ref), channel_id=1, source_target_pairs={{0,1},{1,2},{2,3},{3,4},{4,5},{5,6},{6,7},{8,9},{9,10},{10,11},{11... | collective-permute-start | bytes 393224 | tf_op jit(solution)/shard_map/ppermute | solution.py:568
  8.5 8.9 %collective-permute-start = (f32[4,64,128]{2,1,0:T(8,128)S(1)}, f32[4,64,128]{2,1,0:T(8,128)S(1)}, u32[]{:S(2)}, u32[]{:S(2)}) collective-permute-start(f32[4,64,128]{2,1,0:T(8,128)S(1)} %get-tuple-element.25), channel_id=1, source_target_pairs={{0,64},{64,128},{128,192},{192,256},{256,320},{320,384},{384,448},... | collective-permute-start | bytes 393224 | tf_op jit(solution)/shard_map/ppermute | solution.py:568
  10.4 7.0 %collective-permute-start.1 = (f32[4,64,128]{2,1,0:T(8,128)S(1)}, f32[4,64,128]{2,1,0:T(8,128)S(1)}, u32[]{:S(2)}, u32[]{:S(2)}) collective-permute-start(f32[4,64,128]{2,1,0:T(8,128)S(1)} %get-tuple-element.27), channel_id=1, source_target_pairs={{0,8},{8,16},{16,24},{24,32},{32,40},{40,48},{48,56},{1,9},{9,17},... | collective-permute-start | bytes 393224 | tf_op jit(solution)/shard_map/ppermute | solution.py:568
  14.4 3.0 %copy-start.1 = (bf16[4,128,384]{2,1,0:T(8,128)(2,1)S(1)}, bf16[4,128,384]{2,1,0:T(8,128)(2,1)}, u32[]{:S(2)}) copy-start(bf16[4,128,384]{2,1,0:T(8,128)(2,1)} %constant.16.clone.mh_ref) | copy-start | bytes 1179652
  14.4 3.0 %copy-start.2 = (bf16[4,128,384]{2,1,0:T(8,128)(2,1)S(1)}, bf16[4,128,384]{2,1,0:T(8,128)(2,1)}, u32[]{:S(2)}) copy-start(bf16[4,128,384]{2,1,0:T(8,128)(2,1)} %constant.17.clone.ml_ref) | copy-start | bytes 1179652
  14.4 3.0 %copy-start.4 = (bf16[2,128,128]{2,1,0:T(8,128)(2,1)S(1)}, bf16[2,128,128]{2,1,0:T(8,128)(2,1)}, u32[]{:S(2)}) copy-start(bf16[2,128,128]{2,1,0:T(8,128)(2,1)} %constant.14.clone.wzh_ref) | copy-start | bytes 196612
  14.4 3.0 %copy-start.5 = (bf16[2,128,128]{2,1,0:T(8,128)(2,1)S(1)}, bf16[2,128,128]{2,1,0:T(8,128)(2,1)}, u32[]{:S(2)}) copy-start(bf16[2,128,128]{2,1,0:T(8,128)(2,1)} %constant.15.clone.wzl_ref) | copy-start | bytes 196612
  14.4 3.0 %copy-start.7 = (f32[8,8,128]{2,1,0:T(8,128)S(1)}, f32[8,8,128]{2,1,0:T(8,128)}, u32[]{:S(2)}) copy-start(f32[8,8,128]{2,1,0:T(8,128)} %constant.13.clone.wc_ref) | copy-start | bytes 98308

commit v3 on v2

--- a/solution.py
+++ b/solution.py
@@ -69,11 +69,11 @@
     return [pl.BlockSpec(memory_space=VMEM)] * n
 
 
-STEP = 8
+STEP = 16
 PARTS = 64 // STEP
 
 
-def faces_kernel(w_hbm, f_hbm, xf_ref, xo_ref, yf_ref, yo_ref, zf_ref, s_ref, t_ref, d_ref, w_ref, f_ref, sem):
+def faces_kernel(w_hbm, f_hbm, xf_ref, xo_ref, yf_ref, yo_ref, zf_ref, zo_ref, s_ref, t_ref, d_ref, w_ref, f_ref, sem):
     def copies(g):
         part = pl.ds(g * STEP, STEP)
         return [
@@ -91,7 +91,7 @@
         for x in (0, 1, 66, 67):
             ref[x, 8:72, :] = jnp.zeros((64, 128), f32)
 
-    def part(g, carry):
+    def part(g):
         for copy in copies(g):
             copy.wait()
         packed_s = jnp.zeros((64, 128), f32)
@@ -114,26 +114,26 @@
             here = (lane >= 4 * i) & (lane < 4 * i + 4)
             packed_s = jnp.where(here, rolled(s, 4 * i + 2), packed_s)
             packed_d = jnp.where(here, rolled(d, 4 * i + 2), packed_d)
-        half, quarter = g // 4, g % 4
-        here = lane // 32 == quarter
-        for i, packed in ((half, packed_s), (2 + half, packed_d)):
-            zf_ref[i] = jnp.where(here, pltpu.roll(packed, 32 * quarter, 1), zf_ref[i])
-        return carry
-
-    lax.fori_loop(0, PARTS, part, 0)
+        for ref, packed in ((zo_ref, packed_s), (zo_ref.at[2:4], packed_d)):
+            half = g // 2
+            ref[half] = packed if g % 2 == 0 else jnp.where(lane < 64, ref[half], rolled(packed, 64))
+
+    for g in range(PARTS):
+        part(g)
     for j in range(2):
         xf_ref[j] = s_ref[64 + j, 8:72, :]
         xf_ref[2 + j] = d_ref[62 + j]
         xo_ref[j] = s_ref[2 + j, 8:72, :]
         xo_ref[2 + j] = d_ref[j]
+        zf_ref[j] = jnp.where(lane % 4 < 2, zo_ref[2 * j], rolled(zo_ref[2 * j + 1], 2))
 
 
 def faces(w, f):
-    shapes = [(4, 64, 128)] * 5 + [(68, 80, 128)] * 2 + [(64, 64, 128)]
+    shapes = [(4, 64, 128)] * 4 + [(2, 64, 128), (4, 64, 128)] + [(68, 80, 128)] * 2 + [(64, 64, 128)]
     return pl.pallas_call(
         faces_kernel,
         in_specs=[pl.BlockSpec(memory_space=pltpu.HBM)] * 2,
-        out_specs=whole(8),
+        out_specs=whole(9),
         out_shape=[jax.ShapeDtypeStruct(s, f32) for s in shapes],
         scratch_shapes=[
             VMEM((64, 64, 128), f32),
@@ -375,8 +375,8 @@
     j = lane % 4
     extra = None
     for h in range(2):
-        s = jnp.where(j < 2, zr_ref[h] - zo_ref[h], zo_ref[h])
-        d = jnp.where(j < 2, zr_ref[2 + h], zo_ref[2 + h])
+        s = jnp.where(j < 2, rolled(zr_ref[0], -2 * h) - zo_ref[h], zo_ref[h])
+        d = jnp.where(j < 2, rolled(zr_ref[1], -2 * h), zo_ref[2 + h])
         slope = jnp.where(j >= 2, rolled(s, 2), 0.0) - jnp.where(j < 2, rolled(s, 126), 0.0)
         slope = slope + 8.0 * (
             jnp.where(j == 1, rolled(s, 127), 0.0) - jnp.where(j == 2, rolled(s, 1), 0.0)
@@ -574,13 +574,13 @@
 
 def per_device(warped_image, fixed_image, fine_control, coarse_control):
     sizes = tuple(lax.axis_size(n) for n in ("gx", "gy", "gz"))
-    xf, xo, yf, yo, zf, s, s8, d = faces(warped_image, fixed_image)
+    xf, xo, yf, yo, zf, zo, s, s8, d = faces(warped_image, fixed_image)
+    yr = shifted_up(yf, "gy")
     zr = shifted_up(zf, "gz")
-    yr = shifted_up(yf, "gy")
     xr = shifted_up(xf, "gx")
     bent_fine, bent_coarse = bend(sizes, fine_control, coarse_control)
     fine, coarse = interior(s, s8, d)
-    chunk, fine = finish(sizes[0], fine, coarse, xr, xo, yr, yo, zr, zf, bent_fine, bent_coarse)
+    chunk, fine = finish(sizes[0], fine, coarse, xr, xo, yr, yo, zr, zo, bent_fine, bent_coarse)
     chunk, fine = x_stage(sizes[1], exchanged(chunk, "gx"), fine)
     chunk, fine = y_stage(sizes[2], exchanged(chunk, "gy"), fine)
     return tuple(z_stage(sizes, exchanged(chunk, "gz"), fine))

time: 68.9 us -> 66.4 us (0.964)
  blocking collectives: 48.5 us -> 46.6 us
    all_to_all x3, blocking collectives: 48.5 us -> 46.6 us  [exchanged(): return lax.all_to_all(chunks, axis, split_axis=0, concat_axis=0, tiled=True)]
where the time goes in v3:
time: 66.4 us; the launch traced here: 66.1 us
  blocking collectives  46.6 us (70%)
  starting transfers between devices  9.69 us (15%)
  Pallas kernels  8.91 us (13%)
  between operations  0.83 us (1%)
    all_to_all x3, blocking collectives, exchanged(): return lax.all_to_all(chunks, axis, split_axis=0, concat_axis=0, tiled=True)  46.6 us
    ppermute x3, starting transfers between devices, shifted_up(): lax.ppermute(values, axis, [(i, i + 1) for i in range(lax.axis_size(axis)...  9.69 us
    pallas_call x1, Pallas kernels, faces(): pl.pallas_call(faces_kernel, in_specs=[pl.BlockSpec(memory_space=pltpu.HB...  2.97 us
    pallas_call x1, Pallas kernels, interior(): pl.pallas_call(interior_kernel, in_specs=whole(4), out_specs=whole(2), ou...  2.94 us
    pallas_call x1, Pallas kernels, z_stage(): pl.pallas_call(functools.partial(z_kernel, nx, ny), in_specs=whole(2), ou...  1.38 us
  transfers between devices with their start and end apart: 3, of which 0 were waited for; matrix products, arithmetic and copies ran while one was open for 0% of the time, Pallas kernels for 5%

profile of v3, /device:TPU:2, one launch (start us, length us, event | category | flops | bytes accessed | tf_op | source)
XLA Modules:
  0.0 66.1 jit_solution(6632961677675907314)
XLA Ops:
  0.6 0.0 copy-start.6
  0.6 0.0 copy-start.3
  0.7 0.0 copy-start.2
  0.7 3.0 %faces.1 = (f32[4,64,128]{2,1,0:T(8,128)S(1)}, f32[4,64,128]{2,1,0:T(8,128)S(1)}, f32[4,64,128]{2,1,0:T(8,128)S(1)}, f32[4,64,128]{2,1,0:T(8,128)S(1)}, f32[2,64...) custom-call(f32[64,64,128]{2,1,0:T(8,128)} %w_hbm.1, ...), custom_call_target="tpu_custom_call" | custom-call | tf_op jit(solution)/shard_map/faces/pallas_call | solution.py:133
  3.6 1.9 %collective-permute-start = (f32[4,64,128]{2,1,0:T(8,128)S(1)}, f32[4,64,128]{2,1,0:T(8,128)S(1)}, u32[]{:S(2)}, u32[]{:S(2)}) collective-permute-start(f32[4,64,128]{2,1,0:T(8,128)S(1)} %get-tuple-element.26), channel_id=1, source_target_pairs={{0,64},{64,128},{128,192},{192,256},{256,320},{320,384},{384,448},... | collective-permute-start | bytes 393224 | tf_op jit(solution)/shard_map/ppermute | solution.py:568
  5.6 3.5 %collective-permute-start.1 = (f32[4,64,128]{2,1,0:T(8,128)S(1)}, f32[4,64,128]{2,1,0:T(8,128)S(1)}, u32[]{:S(2)}, u32[]{:S(2)}) collective-permute-start(f32[4,64,128]{2,1,0:T(8,128)S(1)} %get-tuple-element.28), channel_id=1, source_target_pairs={{0,8},{8,16},{16,24},{24,32},{32,40},{40,48},{48,56},{1,9},{9,17},... | collective-permute-start | bytes 393224 | tf_op jit(solution)/shard_map/ppermute | solution.py:568
  9.1 4.3 %collective-permute-start.2 = (f32[2,64,128]{2,1,0:T(8,128)S(1)}, f32[2,64,128]{2,1,0:T(8,128)S(1)}, u32[]{:S(2)}, u32[]{:S(2)}) collective-permute-start(f32[2,64,128]{2,1,0:T(8,128)S(1)} %get-tuple-element.30), channel_id=1, source_target_pairs={{0,1},{1,2},{2,3},{3,4},{4,5},{5,6},{6,7},{8,9},{9,10},{10,11},{11... | collective-permute-start | bytes 196616 | tf_op jit(solution)/shard_map/ppermute | solution.py:568
  13.4 0.0 copy-done.3
  13.4 0.0 copy-done.2
  13.4 0.4 bend.1
  13.8 0.0 copy-done.6
  13.8 0.0 copy-start
  13.8 0.0 copy-start.1
  13.9 0.0 copy-start.4
  13.9 0.0 copy-start.5
  13.9 0.0 copy-start.7
  13.9 2.9 %interior.1 = (f32[12,48,128]{2,1,0:T(8,128)S(1)}, f32[6,24,128]{2,1,0:T(8,128)S(1)}) custom-call(f32[68,80,128]{2,1,0:T(8,128)S(1)} %get-tuple-element.21.s_ref, f32[68,80,128]{2,1,0:T(8,128)S(1)} %get-tuple-element.22.t_ref, f32[64,64,128]{2,1,0:T(8,128)S(1)} %get-tuple-element.23.d_ref, bf16[48,128]{1,0:T(8,128)(2,1)S(1)} %copy-done.6), custom_call_target="tpu_custom_call" | custom-call | flops 40000000 | bytes 4000000 | tf_op jit(solution)/shard_map/interior/pallas_call | solution.py:307
  16.8 0.0 collective-permute-done.2.zr_ref
  16.8 0.0 collective-permute-done.xr_ref
  16.9 0.0 collective-permute-done.1.yr_ref
  16.9 0.0 copy-done
  16.9 0.0 copy-done.1
  16.9 0.0 copy-done.4
  16.9 0.0 copy-done.5
  16.9 0.0 copy-done.7
  16.9 0.9 %finish.1 = (f32[8,48,128]{2,1,0:T(8,128)S(1)}, f32[48,256]{1,0:T(8,128)S(1)}) custom-call(f32[12,48,128]{2,1,0:T(8,128)S(1)} %get-tuple-element.24.af_ref, f32[6,24,128]{2,1,0:T(8,128)S(1)} %get-tuple-element.25.ac_ref, f32[4,64,128]{2,1,0:T(8,128)S(1)} %collective-permute-done.xr_ref, f32[4,64,128]{2,1,0:T(8,128)S(1)} %get-tuple-element.27.xo_ref, ...), custom_call_target="tpu_custom_call" | custom-call | tf_op jit(solution)/shard_map/finish/pallas_call | solution.py:406
  17.8 10.3 %all_to_all.15.got_ref = f32[8,48,128]{2,1,0:T(8,128)S(1)} all-to-all(f32[8,48,128]{2,1,0:T(8,128)S(1)} %get-tuple-element.34), channel_id=1, replica_groups=mesh['gx'=8,'gy'=8,'gz'=8] {'gx'}, dimensions={0} | all-to-all | bytes 393216 | tf_op jit(solution)/shard_map/all_to_all | solution.py:572
  28.2 0.1 xstage.1
  28.3 16.2 %all_to_all.16.got_ref = f32[8,48,128]{2,1,0:T(8,128)S(1)} all-to-all(f32[8,48,128]{2,1,0:T(8,128)S(1)} %get-tuple-element.36), channel_id=1, replica_groups=mesh['gx'=8,'gy'=8,'gz'=8] {'gy'}, dimensions={0} | all-to-all | bytes 393216 | tf_op jit(solution)/shard_map/all_to_all | solution.py:572
  44.5 0.2 ystage.1
  44.6 20.1 %all_to_all.17.got_ref = f32[8,56,128]{2,1,0:T(8,128)S(1)} all-to-all(f32[8,56,128]{2,1,0:T(8,128)S(1)} %get-tuple-element.38), channel_id=1, replica_groups=mesh['gx'=8,'gy'=8,'gz'=8] {'gz'}, dimensions={0} | all-to-all | bytes 458752 | tf_op jit(solution)/shard_map/all_to_all | solution.py:572
  64.7 1.4 %zstage.1 = (f32[3,8,8,16]{3,2,1,0:T(8,128)}, f32[3,16,16,32]{3,2,1,0:T(8,128)}) custom-call(f32[8,56,128]{2,1,0:T(8,128)S(1)} %all_to_all.17.got_ref, f32[48,256]{1,0:T(8,128)S(1)} %get-tuple-element.39.fine_ref), custom_call_target="tpu_custom_call" | custom-call | tf_op jit(solution)/shard_map/zstage/pallas_call | solution.py:554
Async XLA Ops:
  0.6 13.2 %copy-start.6 = (bf16[48,128]{1,0:T(8,128)(2,1)S(1)}, bf16[48,128]{1,0:T(8,128)(2,1)}, u32[]{:S(2)}) copy-start(bf16[48,128]{1,0:T(8,128)(2,1)} %constant.12.clone.left_ref) | copy-start | bytes 36868
  0.6 12.7 %copy-start.3 = (f32[3,8,8,16]{3,2,1,0:T(8,128)S(1)}, f32[3,8,8,16]{3,2,1,0:T(8,128)}, u32[]{:S(2)}) copy-start(f32[3,8,8,16]{3,2,1,0:T(8,128)} %c_ref.1) | copy-start | bytes 36868
  0.7 12.7 %copy-start.2 = (f32[3,16,16,32]{3,2,1,0:T(8,128)S(1)}, f32[3,16,16,32]{3,2,1,0:T(8,128)}, u32[]{:S(2)}) copy-start(f32[3,16,16,32]{3,2,1,0:T(8,128)} %k_ref.1) | copy-start | bytes 294916
  3.6 13.2 %collective-permute-start = (f32[4,64,128]{2,1,0:T(8,128)S(1)}, f32[4,64,128]{2,1,0:T(8,128)S(1)}, u32[]{:S(2)}, u32[]{:S(2)}) collective-permute-start(f32[4,64,128]{2,1,0:T(8,128)S(1)} %get-tuple-element.26), channel_id=1, source_target_pairs={{0,64},{64,128},{128,192},{192,256},{256,320},{320,384},{384,448},... | collective-permute-start | bytes 393224 | tf_op jit(solution)/shard_map/ppermute | solution.py:568
  5.6 11.3 %collective-permute-start.1 = (f32[4,64,128]{2,1,0:T(8,128)S(1)}, f32[4,64,128]{2,1,0:T(8,128)S(1)}, u32[]{:S(2)}, u32[]{:S(2)}) collective-permute-start(f32[4,64,128]{2,1,0:T(8,128)S(1)} %get-tuple-element.28), channel_id=1, source_target_pairs={{0,8},{8,16},{16,24},{24,32},{32,40},{40,48},{48,56},{1,9},{9,17},... | collective-permute-start | bytes 393224 | tf_op jit(solution)/shard_map/ppermute | solution.py:568
  9.1 7.8 %collective-permute-start.2 = (f32[2,64,128]{2,1,0:T(8,128)S(1)}, f32[2,64,128]{2,1,0:T(8,128)S(1)}, u32[]{:S(2)}, u32[]{:S(2)}) collective-permute-start(f32[2,64,128]{2,1,0:T(8,128)S(1)} %get-tuple-element.30), channel_id=1, source_target_pairs={{0,1},{1,2},{2,3},{3,4},{4,5},{5,6},{6,7},{8,9},{9,10},{10,11},{11... | collective-permute-start | bytes 196616 | tf_op jit(solution)/shard_map/ppermute | solution.py:568
  13.8 3.0 %copy-start = (bf16[4,128,384]{2,1,0:T(8,128)(2,1)S(1)}, bf16[4,128,384]{2,1,0:T(8,128)(2,1)}, u32[]{:S(2)}) copy-start(bf16[4,128,384]{2,1,0:T(8,128)(2,1)} %constant.16.clone.mh_ref) | copy-start | bytes 1179652
  13.8 3.0 %copy-start.1 = (bf16[4,128,384]{2,1,0:T(8,128)(2,1)S(1)}, bf16[4,128,384]{2,1,0:T(8,128)(2,1)}, u32[]{:S(2)}) copy-start(bf16[4,128,384]{2,1,0:T(8,128)(2,1)} %constant.17.clone.ml_ref) | copy-start | bytes 1179652
  13.9 3.0 %copy-start.4 = (bf16[2,128,128]{2,1,0:T(8,128)(2,1)S(1)}, bf16[2,128,128]{2,1,0:T(8,128)(2,1)}, u32[]{:S(2)}) copy-start(bf16[2,128,128]{2,1,0:T(8,128)(2,1)} %constant.14.clone.wzh_ref) | copy-start | bytes 196612
  13.9 3.0 %copy-start.5 = (bf16[2,128,128]{2,1,0:T(8,128)(2,1)S(1)}, bf16[2,128,128]{2,1,0:T(8,128)(2,1)}, u32[]{:S(2)}) copy-start(bf16[2,128,128]{2,1,0:T(8,128)(2,1)} %constant.15.clone.wzl_ref) | copy-start | bytes 196612
  13.9 3.0 %copy-start.7 = (f32[8,8,128]{2,1,0:T(8,128)S(1)}, f32[8,8,128]{2,1,0:T(8,128)}, u32[]{:S(2)}) copy-start(f32[8,8,128]{2,1,0:T(8,128)} %constant.13.clone.wc_ref) | copy-start | bytes 98308
